TPU v7x, 32 devices: a whole 2x2x4 slice. The times are simulated.
32 devices in a mesh: gx: 8 (over z, y), gy: 4 (over x, core).
Axes of the slice: x: 2, y: 2, z: 4, core: 2. Of those that a mesh axis runs over, the one named last changes fastest.
Arguments:
- image_feats: bfloat16 [16384, 4096], P('gx', 'gy'), may hold values from -6 to 6
- w_kv: bfloat16 [4096, 2048], P('gy'), may hold values from -0.09375 to 0.09375
- k_gain: float32 [128], replicated, may hold values from 0.25 to 1.75
- tile_rows: int32 [128], replicated, may hold values from 0 to 128
- deal: int32 [8, 16], replicated, may hold values from 0 to 127, as said below
Outputs:
- keys_out: bfloat16 [16384, 1024], P('gx', 'gy')
- values_out: bfloat16 [16384, 1024], P('gx', 'gy')
Inputs may be any that keep to these rules, and one draw needn't show every extreme that they name: Each input tile is named exactly once; deal[j, s] % 16 == s; two entries of one row j that name tiles of the same index of gx stand in columns s that differ by a multiple of 8, so one row names at most 2 tiles of one index of gx, and exactly 2 for some.
All inputs are finite; a program needn't handle non-finite values.
Results may differ from a plain program's by a relative error of at most 0.001.
Values may be sent and summed in bfloat16 or wider, within the bound.
No kernel may reach another device: no remote copies, remote signals or barrier semaphores. Data moves between devices by JAX's collectives and lax.ppermute only.
A program may use at most 128 MiB of HBM per device.

v0:
```python
import jax
import jax.numpy as jnp
from jax import lax
from jax.sharding import PartitionSpec as P

HD = 128
TILE = 128
TPD = 16


epsilon = 1e-05


def local(image_feats, w_kv, k_gain, tile_rows, deal):
    local_width = image_feats.shape[1]
    groups = lax.axis_size("gx")
    own_index = lax.axis_index("gx")
    slots = max(1, TPD // groups)
    wanted = lax.dynamic_index_in_dim(deal, own_index, 0, keepdims=False)
    slot_index = jnp.arange(TPD, dtype=jnp.int32)
    slot_class = slot_index // groups
    places = jnp.arange(slots, dtype=jnp.int32)
    class_match = slot_class[None, :] == places[:, None]
    own_tiles = own_index * TPD + slot_index
    sending = deal == own_tiles[None, :]
    send_select = (sending[:, None, :] & class_match[None, :, :]).astype(jnp.bfloat16)
    blocks = image_feats.reshape(TPD, TILE, local_width)
    outgoing = jnp.einsum(
        "dcs,str->dctr", send_select, blocks, preferred_element_type=jnp.float32
    ).astype(jnp.bfloat16)
    incoming = lax.all_to_all(outgoing, "gx", split_axis=0, concat_axis=0, tiled=True)
    sources = jnp.arange(groups, dtype=jnp.int32)
    from_source = (wanted // TPD)[:, None] == sources[None, :]
    take_select = (from_source[:, :, None] & class_match.T[:, None, :]).astype(jnp.bfloat16)
    dealt_tiles = jnp.einsum(
        "snc,nctr->str", take_select, incoming, preferred_element_type=jnp.float32
    ).astype(jnp.bfloat16)
    row_count = TPD * TILE
    dealt_rows = dealt_tiles.reshape(row_count, local_width)
    total_kv = w_kv.shape[1] // 2
    partial_value = jnp.dot(dealt_rows, w_kv, preferred_element_type=jnp.float32)
    projected = lax.psum_scatter(
        partial_value.reshape(row_count, 2, total_kv), "gy", scatter_dimension=2, tiled=True
    )
    share_cols = projected.shape[2]
    key_pre = projected[:, 0, :].reshape(row_count, share_cols // HD, HD)
    value_pre = projected[:, 1, :]
    mean_square = jnp.mean(key_pre * key_pre, axis=-1, keepdims=True)
    normed = (key_pre * lax.rsqrt(mean_square + epsilon) * k_gain).reshape(row_count, share_cols)
    all_tiles = jnp.arange(tile_rows.shape[0], dtype=jnp.int32)
    limits = jnp.sum(
        jnp.where(wanted[:, None] == all_tiles[None, :], tile_rows[None, :], 0), axis=1
    )
    position = jnp.arange(TILE, dtype=jnp.int32)
    valid_rows = (position[None, :] < limits[:, None]).reshape(row_count, 1)
    keys_out = jnp.where(valid_rows, normed, 0.0).astype(jnp.bfloat16)
    values_out = jnp.where(valid_rows, value_pre, 0.0).astype(jnp.bfloat16)
    return (keys_out, values_out)


def solution(mesh):
    placed = (P("gx", "gy"), P("gy", None), P(), P(), P())
    return jax.shard_map(
        local, mesh=mesh, in_specs=placed, out_specs=(P("gx", "gy"), P("gx", "gy")), check_vma=False
    )
```

profile of v0, /device:TPU:0, one launch (start us, length us, event | category | flops | bytes accessed | tf_op | source)
XLA Modules:
  0.0 287.5 jit_solution(783638681754824455)
XLA Ops:
  7.2 0.0 copy-start
  7.2 0.7 broadcast_compare_fusion
  7.9 5.1 %fusion.6 = bf16[8,2,128,1024]{3,0,1,2:T(8,128)(2,1)S(1)} fusion(bf16[16,128,1024,1]{2,1,0,3:T(8,128)(2,1)} %bitcast.46, pred[2,16]{1,0:T(4,128)(4,1)S(1)} %iota_compare_fusion.3, pred[8,16]{1,0:T(8,128)(4,1)S(1)} %broadcast_compare_fusion), kind=kOutput, calls=%fused_computation.5 | convolution fusion | flops 69206272 | bytes 8388768 | tf_op jit(solution)/shard_map/dcs,str->dctr/dot_general | solution.py:28
  13.0 6.3 %copy.27 = bf16[8,2,128,1024]{3,1,2,0:T(2,128)(2,1)} copy(bf16[8,2,128,1024]{3,0,1,2:T(8,128)(2,1)S(1)} %fusion.6) | data formatting | bytes 8388608 | tf_op jit(solution)/shard_map/convert_element_type | solution.py:30
  19.3 7.3 %all-to-all-start = ((bf16[8,2,128,1024]{3,1,2,0:T(2,128)(2,1)}), bf16[8,2,128,1024]{3,1,2,0:T(2,128)(2,1)}, u32[]{:S(2)}, u32[]{:S(2)}) async-start(bf16[8,2,128,1024]{3,1,2,0:T(2,128)(2,1)} %copy.27), calls=%async_computation | async-start | bytes 8388608 | tf_op jit(solution)/shard_map/all_to_all | solution.py:31
  26.6 0.2 reduce-scatter.2.cloned.1.call-start
  26.9 6.4 %copy.37 = bf16[2048,1024]{1,0:T(8,128)(2,1)} copy(bf16[2048,1024]{0,1:T(8,128)(2,1)} %bitcast.47) | data formatting | bytes 8388608 | tf_op jit(solution)/shard_map/dot_general | solution.py:41
  33.3 0.7 and_select_fusion.1
  34.0 85.9 %all-to-all-done = bf16[8,2,128,1024]{3,1,2,0:T(2,128)(2,1)} async-done(((bf16[8,2,128,1024]{3,1,2,0:T(2,128)(2,1)}), bf16[8,2,128,1024]{3,1,2,0:T(2,128)(2,1)}, u32[]{:S(2)}, u32[]{:S(2)}) %all-to-all-start) | async-done | bytes 4194336 | tf_op jit(solution)/shard_map/all_to_all | solution.py:31
  119.9 4.7 %bitcast_convert_fusion = bf16[16,128,1024]{2,0,1:T(8,128)(2,1)S(1)} fusion(bf16[8,2,128,1024]{3,1,2,0:T(2,128)(2,1)} %all-to-all-done, pred[16,2]{0,1:T(4,128)(4,1)S(1)} %iota_compare_fusion.4, pred[16,8]{0,1:T(8,128)(4,1)S(1)} %iota_compare_fusion.2), kind=kOutput, calls=%fused_computation | convolution fusion | flops 69206272 | bytes 8388768 | tf_op jit(solution)/shard_map/snc,nctr->str/dot_general | solution.py:35
  124.6 0.0 copy-start.2
  124.7 2.3 copy.29
  127.0 0.0 copy-done.2
  127.0 11.7 %fusion.23 = f32[2048,2,1024]{2,0,1:T(8,128)} fusion(bf16[2048,1024,1]{1,0,2:T(8,128)(2,1)S(1)} %bitcast.49, bf16[2,1024,1024]{2,1,0:T(8,128)(2,1)S(1)} %bitcast.48), kind=kOutput, calls=%fused_computation.42 | convolution fusion | flops 8589934592 | bytes 25165824 | tf_op jit(solution)/shard_map/dot_general | solution.py:41
  138.7 0.0 copy-start.3
  138.8 0.0 reduce-scatter.2.cloned.1.call-update
  138.8 0.6 copy-done.3
  139.4 0.2 select_reduce_fusion
  139.6 0.0 copy-done
  139.6 0.1 fusion.14
  139.7 123.2 %reduce-scatter.2.cloned.1.call-done = f32[2048,2,256]{2,0,1:T(8,128)} async-done(((f32[2048,2,1024]{2,0,1:T(8,128)}), f32[2048,2,256]{2,0,1:T(8,128)}) %reduce-scatter.2.cloned.1.call-update) | async-done | bytes 4194320 | tf_op jit(solution)/shard_map/reduce_scatter | solution.py:42
  262.9 3.1 %slice_multiply_fusion = f32[2048,1,256]{2,0,1:T(8,128)} fusion(f32[2048,2,256]{2,0,1:T(8,128)} %reduce-scatter.2.cloned.1.call-done), kind=kLoop, calls=%fused_computation.13 | loop fusion | flops 524288 | bytes 4194304 | tf_op jit(solution)/shard_map/mul | solution.py:48
  265.9 2.3 mul.39
  268.2 3.5 %reduce_sum.19 = f32[2048,2]{1,0:T(8,128)S(1)} reduce(f32[2048,2,128]{2,1,0:T(2,128)S(1)} %mul.39, f32[]{:T(128)} %constant.46.clone.1), dimensions={2}, to_apply=%region_2.3 | reduce | flops 520192 | bytes 2113540 | tf_op jit(solution)/shard_map/reduce_sum | solution.py:48
  271.7 0.0 copy-start.1
  271.7 0.1 add_rsqrt_fusion
  271.9 2.7 fusion.13
  274.6 4.6 %mul.40 = f32[2048,2,128]{2,1,0:T(2,128)S(1)} broadcast(f32[2048,2]{1,0:T(8,128)S(1)} %add_rsqrt_fusion), dimensions={0,1} | broadcast | bytes 2113536 | tf_op jit(solution)/shard_map/mul | solution.py:49
  279.2 0.0 copy-done.1
  279.2 1.4 fusion.11
  (6 shorter events, 0.0 us)
Async XLA Ops:
  7.2 132.4 %copy-start = (f32[128]{0:T(128)S(1)}, f32[128]{0:T(128)}, u32[]{:S(2)}) copy-start(f32[128]{0:T(128)} %param.7) | copy-start | bytes 1540
  19.3 100.6 %all-to-all-start = ((bf16[8,2,128,1024]{3,1,2,0:T(2,128)(2,1)}), bf16[8,2,128,1024]{3,1,2,0:T(2,128)(2,1)}, u32[]{:S(2)}, u32[]{:S(2)}) async-start(bf16[8,2,128,1024]{3,1,2,0:T(2,128)(2,1)} %copy.27), calls=%async_computation | async-start | bytes 8388608 | tf_op jit(solution)/shard_map/all_to_all | solution.py:31
  26.6 236.2 %reduce-scatter.2.cloned.1.call-start = ((), (), s32[]{:S(2)}) async-start(), calls=%async_computation.2 | async-start | bytes 20971520 | tf_op jit(solution)/shard_map/reduce_scatter | solution.py:42
  124.6 2.3 copy-start.2
  138.7 0.7 copy-start.3
  271.7 7.5 %copy-start.1 = (f32[2048,2,256]{2,0,1:T(8,128)S(1)}, f32[2048,2,256]{2,0,1:T(8,128)}, u32[]{:S(2)}) copy-start(f32[2048,2,256]{2,0,1:T(8,128)} %reduce-scatter.2.cloned.1.call-done) | copy-start | bytes 12582916
Sparse Core Ops, SparseCore 0:
  138.9 123.9 reduce-scatter.1
where the time goes:
time: 288 us; the launch traced here: 287 us
  waiting for transfers between devices  209 us (73%)
  local copies, waits for them, and re-layouts  22.6 us (8%)
  matrix products  21.6 us (8%)
  between operations  14.2 us (5%)
  other arithmetic  12.4 us (4%)
  starting transfers between devices  7.53 us (3%)
    reduce_scatter x1, waiting for transfers between devices, local(): lax.psum_scatter(partial_value.reshape(row_count, 2, total_kv), 'gy', sca...  123 us
    all_to_all x1, waiting for transfers between devices, local(): lax.all_to_all(outgoing, 'gx', split_axis=0, concat_axis=0, tiled=True)  85.9 us
    dot_general x1, matrix products, local(): jnp.dot(dealt_rows, w_kv, preferred_element_type=jnp.float32)  11.7 us
    all_to_all x1, starting transfers between devices, local(): lax.all_to_all(outgoing, 'gx', split_axis=0, concat_axis=0, tiled=True)  7.31 us
    dot_general x1, local copies, waits for them, and re-layouts, local(): jnp.dot(dealt_rows, w_kv, preferred_element_type=jnp.float32)  6.41 us
    convert_element_type x1, local copies, waits for them, and re-layouts, local(): outgoing = jnp.einsum('dcs,str->dctr', send_select, blocks, preferred_ele...  6.27 us
  transfers between devices with their start and end apart: 2, of which 2 were waited for; matrix products, arithmetic and copies ran while one was open for 3% of the time, Pallas kernels for 0%

commit v1 on v0

v1 whole, which is shorter than its diff:
```python
import functools

import jax
import jax.numpy as jnp
from jax import lax
from jax.experimental import pallas as pl
from jax.experimental.pallas import tpu as pltpu
from jax.sharding import PartitionSpec as P


HD = 128
TILE = 128
TPD = 16
CORES = 2
epsilon = 1e-05

STEPS = 64.0
TOP = 32700.0
PAD = 16

VMEM = pl.BlockSpec(memory_space=pltpu.VMEM)
SMEM = pl.BlockSpec(memory_space=pltpu.SMEM)
ANY = pl.BlockSpec(memory_space=pl.ANY)


def call(body, ins, outs, shapes, flops, scratch=()):
    nbytes = sum(s.size * s.dtype.itemsize for s in shapes)
    return pl.pallas_call(
        body,
        in_specs=ins,
        out_specs=outs,
        out_shape=shapes,
        scratch_shapes=scratch,
        cost_estimate=pl.CostEstimate(flops=int(flops), bytes_accessed=2 * nbytes, transcendentals=0),
    )


STAGES = ((3, "a2a"), (3, "permute"), (2, "a2a"))


def target(k):
    chips = lax.axis_size("gy") // CORES
    member = lax.axis_index("gy")
    chip, core = member // CORES, member % CORES
    there = (chip + k) % chips * CORES
    return there + core, there + 1 - core


def run_all(copies):
    for c in copies:
        c.start()
    for c in copies:
        c.wait()


def prepare_body(f_ref, w_ref, *refs, stages, ks, share):
    feats, weights, sem = refs[: len(stages)], refs[len(stages) : -1], refs[-1]
    members = lax.axis_size("gy")
    copies = []
    for i, k in enumerate(ks):
        for j, which in enumerate(target(k)):
            w_out = weights[2 * i + j]
            for part in range(2):
                start = pl.multiple_of((part * members + which) * share, share)
                copies.append((w_ref.at[:, pl.ds(start, share)], w_out.at[:, part * share : (part + 1) * share]))
    for (r, m), f_out in zip(stages, feats):
        copies.append((f_ref.at[:, r : r + m], f_out))
    run_all([pltpu.make_async_copy(a, b, sem.at[i]) for i, (a, b) in enumerate(copies)])


def prepare(feats, w_kv, stages, ks, share):
    width = feats.shape[2]
    shapes = [jax.ShapeDtypeStruct((TPD, m, width), feats.dtype) for _, m in stages]
    shapes += [jax.ShapeDtypeStruct((width, 2 * share), w_kv.dtype) for _ in range(2 * len(ks))]
    body = functools.partial(prepare_body, stages=stages, ks=ks, share=share)
    sems = [pltpu.SemaphoreType.DMA((len(stages) + 4 * len(ks),))]
    got = call(body, [ANY, ANY], [VMEM] * len(shapes), shapes, 1e6, sems)(feats, w_kv)
    weights = got[len(stages) :]
    return got[: len(stages)], weights[::2], weights[1::2]


def encode(total, out_ref, share):
    rows = total.shape[0]
    lane = lax.broadcasted_iota(jnp.int32, (rows, HD), 1)
    line = lax.broadcasted_iota(jnp.int32, (PAD, HD), 0)
    heads = 2 * share // HD
    codes = jnp.zeros((rows, HD), jnp.float32)
    for h in range(heads):
        one = total[:, h * HD : (h + 1) * HD]
        top = jnp.max(jnp.abs(one), axis=1, keepdims=True)
        code = jnp.ceil(jnp.log2(jnp.maximum(top, 1e-30)) * STEPS) + 1.0
        factor = TOP * jnp.exp2(code * (-1.0 / STEPS))
        scaled = jnp.floor(one * factor + 0.5)
        out_ref[0:rows, h * HD : (h + 1) * HD] = scaled.astype(jnp.int32).astype(jnp.int16)
        codes = jnp.where(lane == h, code, codes)
    kept = [jnp.zeros((PAD, HD), jnp.float32) for _ in range(heads)]
    for g in range(rows // HD):
        turned = codes[g * HD : (g + 1) * HD, :].T
        for h in range(heads):
            kept[h] = jnp.where(line == g, turned[h : h + 1, :], kept[h])
    for h in range(heads):
        out_ref[rows : rows + PAD, h * HD : (h + 1) * HD] = kept[h].astype(jnp.int32).astype(jnp.int16)


def project_body(*refs, jobs, share):
    outs = refs[-len(jobs) :]
    for (f, r, fp, w, wp, far), out_ref in zip(jobs, outs):
        m = refs[fp].shape[1]
        width = refs[fp].shape[2]
        own = refs[f][:, r : r + m, :].reshape(TPD * m, width)
        other = refs[fp][...].reshape(TPD * m, width)
        total = jnp.dot(own, refs[w][...], preferred_element_type=jnp.float32)
        total += jnp.dot(other, refs[wp][...], preferred_element_type=jnp.float32)
        if far:
            encode(total, out_ref, share)
        else:
            out_ref[...] = total


def project(feats, jobs, share):
    inputs, listed, shapes = [feats], [], []

    def at(x):
        for i, y in enumerate(inputs):
            if x is y:
                return i
        inputs.append(x)
        return len(inputs) - 1

    flops = 0
    for (r, m), block, w, wp, far in jobs:
        rows = TPD * m
        listed.append((0, r, at(block), at(w), at(wp), far))
        shape = ((rows + PAD, 2 * share), jnp.int16) if far else ((rows, 2 * share), jnp.float32)
        shapes.append(jax.ShapeDtypeStruct(*shape))
        flops += 8 * rows * feats.shape[2] * share
    return call(
        functools.partial(project_body, jobs=listed, share=share),
        [VMEM] * len(inputs),
        [VMEM] * len(jobs),
        shapes,
        flops,
    )(*inputs)


def finish_body(deal_ref, limit_ref, gain_ref, own_ref, *rest, stage, share, peers, span, mode):
    r0, m = stage
    rows = TPD * m
    groups = lax.axis_size("gx")
    own_index = lax.axis_index("gx")
    codes, outs, scale_ref = rest[:peers], rest[peers:-1], rest[-1]
    heads = 2 * share // HD
    line = lax.broadcasted_iota(jnp.int32, (HD, HD), 0)
    for p in range(peers):
        saved = codes[p][rows : rows + PAD, :].astype(jnp.int32).astype(jnp.float32)
        for g in range(rows // HD):
            stack = jnp.zeros((HD, HD), jnp.float32)
            for h in range(heads):
                stack = jnp.where(line == h, saved[g : g + 1, h * HD : (h + 1) * HD], stack)
            scale_ref[p, g * HD : (g + 1) * HD, :] = jnp.exp2(stack.T * (1.0 / STEPS)) * (1.0 / TOP)
    gain = gain_ref[...]
    position = r0 + lax.broadcasted_iota(jnp.int32, (m, HD), 0)
    first = own_index * TPD
    for k in range(groups):
        taker = k if mode == "a2a" else (own_index + k) % groups
        out = outs[0].at[k] if mode == "a2a" else outs[k]
        for c in range(TPD // span):
            tile = c * span
            for t in range(c * span, (c + 1) * span):
                tile = jnp.where(deal_ref[taker, t] == first + t, t, tile)
            inside = position < limit_ref[first + tile]
            start = pl.multiple_of(tile * m, 16)
            for h in range(heads):
                cols = slice(h * HD, (h + 1) * HD)
                total = own_ref[pl.ds(start, m), cols]
                for p in range(peers):
                    code = codes[p][pl.ds(start, m), cols].astype(jnp.int32).astype(jnp.float32)
                    total += code * scale_ref[p, pl.ds(start, m), h : h + 1]
                if h < heads // 2:
                    mean_square = jnp.mean(total * total, axis=1, keepdims=True)
                    total = total * lax.rsqrt(mean_square + epsilon) * gain
                out[c * m : (c + 1) * m, cols] = jnp.where(inside, total, 0.0).astype(jnp.bfloat16)


def finish(stage, deal, tile_rows, gain, own, codes, groups, share, span, mode):
    rows = TPD * stage[1]
    shape = (TPD // span * stage[1], 2 * share)
    if mode == "a2a":
        shapes = [jax.ShapeDtypeStruct((groups,) + shape, jnp.bfloat16)]
    else:
        shapes = [jax.ShapeDtypeStruct(shape, jnp.bfloat16)] * groups
    body = functools.partial(
        finish_body, stage=stage, share=share, peers=len(codes), span=span, mode=mode
    )
    return call(
        body,
        [SMEM, SMEM, VMEM, VMEM] + [VMEM] * len(codes),
        [VMEM] * len(shapes),
        shapes,
        40 * rows * share,
        [pltpu.VMEM((max(1, len(codes)), rows, HD), jnp.float32)],
    )(deal, tile_rows, gain, own, *codes)


def place_body(deal_ref, *refs, stages, modes, share, span):
    groups = lax.axis_size("gx")
    own_index = lax.axis_index("gx")
    pieces, (keys_ref, values_ref, sem) = list(refs[:-3]), refs[-3:]
    todo = []
    for s, ((r0, m), mode) in enumerate(zip(stages, modes)):
        whole = pieces.pop(0) if mode == "a2a" else None
        for k in range(groups):
            giver = k if mode == "a2a" else (own_index - k + groups) % groups
            piece = whole.at[k] if mode == "a2a" else pieces.pop(0)
            for c in range(TPD // span):
                slot = -1
                for t in range(c * span, (c + 1) * span):
                    slot = jnp.where(deal_ref[own_index, t] // TPD == giver, t, slot)
                row = pl.multiple_of(jnp.maximum(slot, 0) * TILE + r0, 16)
                for i, ref in enumerate((keys_ref, values_ref)):
                    copy = pltpu.make_async_copy(
                        piece.at[c * m : (c + 1) * m, i * share : (i + 1) * share],
                        ref.at[pl.ds(row, m)],
                        sem.at[s, k, c, i],
                    )
                    todo.append((slot, copy))
    for slot, copy in todo:
        pl.when(slot >= 0)(copy.start)
    for slot, copy in todo:
        pl.when(slot >= 0)(copy.wait)


def place(stages, modes, deal, pieces, groups, share, span):
    shape = jax.ShapeDtypeStruct((TPD * TILE, share), jnp.bfloat16)
    return call(
        functools.partial(place_body, stages=stages, modes=modes, share=share, span=span),
        [SMEM] + [VMEM] * len(pieces),
        [ANY, ANY],
        [shape, shape],
        1e6,
        [pltpu.SemaphoreType.DMA((len(stages), groups, TPD // span, 2))],
    )(deal, *pieces)


def local(image_feats, w_kv, k_gain, tile_rows, deal):
    groups = lax.axis_size("gx")
    members = lax.axis_size("gy")
    chips = members // CORES
    share = w_kv.shape[1] // 2 // members
    feats = image_feats.reshape(TPD, TILE, image_feats.shape[1])
    gain = k_gain.reshape(1, HD)
    span = min(TPD, groups)
    stages, modes, row = [], [], 0
    for units, mode in STAGES:
        stages.append((row * 16, units * 16))
        modes.append(mode)
        row += units

    def swap(x):
        return lax.ppermute(x, "gy", [(g, g ^ 1) for g in range(members)])

    def along(x, k):
        pairs = [
            (x0 * CORES + c, (x0 + k) % chips * CORES + c) for x0 in range(chips) for c in range(CORES)
        ]
        return lax.ppermute(x, "gy", pairs)

    n = len(stages)
    f0, w_far, w_send = prepare(feats, w_kv, stages[:1], range(1, chips), share)
    v_far = [swap(w) for w in w_send]
    near = [swap(f) for f in f0]
    f1, (w_near,), w_send = prepare(feats, w_kv, stages[1:], (0,), share)
    near += [swap(f) for f in f1]
    v_near = swap(w_send[0])

    def far_jobs(s):
        return [(stages[s], near[s], w_far[k], v_far[k], True) for k in range(chips - 1)]

    def own_job(s):
        return [(stages[s], near[s], w_near, v_near, False)]

    codes, own = [None] * n, [None] * n
    for s in range(n):
        jobs = far_jobs(s) + (own_job(s - 1) if s else []) + (own_job(s) if s == n - 1 else [])
        got = project(feats, jobs, share)
        codes[s] = [along(x, k + 1) for k, x in enumerate(got[: chips - 1])]
        if s:
            own[s - 1] = got[chips - 1]
            own[s] = got[-1]
    pieces = []
    for s in range(n):
        laid = finish(
            stages[s], deal, tile_rows, gain, own[s], codes[s], groups, share, span, modes[s]
        )
        if modes[s] == "a2a":
            pieces.append(lax.all_to_all(laid[0], "gx", 0, 0, tiled=True))
            continue
        for k, x in enumerate(laid):
            pairs = [(i, (i + k) % groups) for i in range(groups)]
            pieces.append(lax.ppermute(x, "gx", pairs) if k else x)
    return tuple(place(stages, modes, deal, pieces, groups, share, span))


def solution(mesh):
    placed = (P("gx", "gy"), P("gy", None), P(), P(), P())

    return jax.shard_map(local, mesh=mesh, in_specs=placed, out_specs=(P("gx", "gy"), P("gx", "gy")), check_vma=False)
```

time: 288 us -> 141 us (0.49)
  the two profiles are of different devices: /device:TPU:0 before, /device:TPU:20 now
where the time goes in v1:
time: 141 us
  Pallas kernels  55.2 us (39%)
  waiting for transfers between devices  54.2 us (38%)
  starting transfers between devices  26.1 us (19%)
  local copies, waits for them, and re-layouts  4.67 us (3%)
    ppermute x3, waiting for transfers between devices, along(): return lax.ppermute(x, 'gy', pairs)  37.3 us
    pallas_call x3, Pallas kernels, project(): call(functools.partial(project_body, jobs=listed, share=share), [VMEM] *...  25.8 us
    pallas_call x3, Pallas kernels, finish(): call(body, [SMEM, SMEM, VMEM, VMEM] + [VMEM] * len(codes), [VMEM] * len(s...  16.9 us
    all_to_all x2, starting transfers between devices, local(): pieces.append(lax.all_to_all(laid[0], 'gx', 0, 0, tiled=True))  12.1 us
    ppermute x7, waiting for transfers between devices, local(): pieces.append(lax.ppermute(x, 'gx', pairs) if k else x)  11.9 us
    pallas_call x2, Pallas kernels, prepare(): call(body, [ANY, ANY], [VMEM] * len(shapes), shapes, 1000000.0, sems)  8.71 us
    ppermute x7, starting transfers between devices, local(): pieces.append(lax.ppermute(x, 'gx', pairs) if k else x)  8.33 us
    ppermute x5, waiting for transfers between devices, swap(): return lax.ppermute(x, 'gy', [(g, g ^ 1) for g in range(members)])  5.04 us
  transfers between devices with their start and end apart: 17, of which 9 were waited for; matrix products, arithmetic and copies ran while one was open for 0% of the time, Pallas kernels for 33%

profile of v1, /device:TPU:20, one launch (start us, length us, event | category | flops | bytes accessed | tf_op | source)
XLA Modules:
  0.0 141.1 jit_solution(8527502577008476071)
XLA Ops:
  0.6 4.7 %shard_map.68 = (bf16[16,48,1024]{2,1,0:T(8,128)(2,1)}, bf16[16,32,1024]{2,1,0:T(8,128)(2,1)}, bf16[1024,512]{1,0:T(8,128)(2,1)}, bf16[1024,512]{1,0:T(8,128)(2,1)}) custom-call(bf16[16,128,1024]{2,1,0:T(8,128)(2,1)} %bitcast.2, bf16[1024,2048]{1,0:T(8,128)(2,1)} %w_ref.3), custom_call_target="tpu_custom_call" | custom-call | flops 1000000 | bytes 9437184 | tf_op jit(solution)/shard_map/pallas_call | solution.py:77
  5.3 0.1 collective-permute-start
  5.4 4.0 %shard_map.69 = (bf16[16,48,1024]{2,1,0:T(8,128)(2,1)}, bf16[1024,512]{1,0:T(8,128)(2,1)}, bf16[1024,512]{1,0:T(8,128)(2,1)}) custom-call(bf16[16,128,1024]{2,1,0:T(8,128)(2,1)} %bitcast.3, bf16[1024,2048]{1,0:T(8,128)(2,1)} %w_ref.3), custom_call_target="tpu_custom_call" | custom-call | flops 1000000 | bytes 7340032 | tf_op jit(solution)/shard_map/pallas_call | solution.py:77
  9.4 0.5 collective-permute-start.1
  10.0 0.1 collective-permute-start.3
  10.0 0.4 collective-permute-start.5
  10.5 0.1 collective-permute-start.2
  10.6 1.9 %collective-permute-done.1.refs_3_ = bf16[1024,512]{1,0:T(8,128)(2,1)S(1)} collective-permute-done((bf16[1024,512]{1,0:T(8,128)(2,1)}, bf16[1024,512]{1,0:T(8,128)(2,1)S(1)}, u32[]{:S(2)}, u32[]{:S(2)}) %collective-permute-start.1) | collective-permute-done | bytes 1048608 | tf_op jit(solution)/shard_map/ppermute | solution.py:260
  12.5 1.6 %collective-permute-done.3.refs_6_ = bf16[1024,512]{1,0:T(8,128)(2,1)} collective-permute-done((bf16[1024,512]{1,0:T(8,128)(2,1)}, bf16[1024,512]{1,0:T(8,128)(2,1)}, u32[]{:S(2)}, u32[]{:S(2)}) %collective-permute-start.3) | collective-permute-done | bytes 1048608 | tf_op jit(solution)/shard_map/ppermute | solution.py:260
  14.1 1.5 %collective-permute-done.5.refs_1_ = bf16[16,32,1024]{2,1,0:T(8,128)(2,1)} collective-permute-done((bf16[16,32,1024]{2,1,0:T(8,128)(2,1)}, bf16[16,32,1024]{2,1,0:T(8,128)(2,1)}, u32[]{:S(2)}, u32[]{:S(2)}) %collective-permute-start.5) | collective-permute-done | bytes 1048608 | tf_op jit(solution)/shard_map/ppermute | solution.py:260
  15.6 0.0 collective-permute-done.refs_1_.refs_4_
  15.6 9.5 %shard_map.73 = (s16[528,512]{1,0:T(8,128)(2,1)}, f32[768,512]{1,0:T(8,128)}, f32[512,512]{1,0:T(8,128)}) custom-call(bf16[16,128,1024]{2,1,0:T(8,128)(2,1)} %bitcast.4, bf16[16,32,1024]{2,1,0:T(8,128)(2,1)} %collective-permute-done.5.refs_1_, bf16[1024,512]{1,0:T(8,128)(2,1)} %get-tuple-element.23.refs_2_, bf16[1024,512]{1,0:T(8,128)(2,1)} %copy-done.3, ...), custom_call_target="tpu_custom_call" | custom-call | flops 3758096384 | bytes 6324224 | tf_op jit(solution)/shard_map/pallas_call | solution.py:137
  25.1 1.5 %collective-permute-start.14 = (s16[528,512]{1,0:T(8,128)(2,1)}, s16[528,512]{1,0:T(8,128)(2,1)S(1)}, u32[]{:S(2)}, u32[]{:S(2)}) collective-permute-start(s16[528,512]{1,0:T(8,128)(2,1)} %get-tuple-element.41), channel_id=1, source_target_pairs={{0,2},{1,3},{2,0},{3,1},{4,6},{5,7},{6,4},{7,5},{8,10},{9,11},{10,... | collective-permute-start | bytes 1622024 | tf_op jit(solution)/shard_map/ppermute | solution.py:266
  26.6 13.3 %collective-permute-done.14.rest_0_ = s16[528,512]{1,0:T(8,128)(2,1)S(1)} collective-permute-done((s16[528,512]{1,0:T(8,128)(2,1)}, s16[528,512]{1,0:T(8,128)(2,1)S(1)}, u32[]{:S(2)}, u32[]{:S(2)}) %collective-permute-start.14) | collective-permute-done | bytes 540704 | tf_op jit(solution)/shard_map/ppermute | solution.py:266
  39.9 0.8 copy-done.6
  40.7 5.2 %shard_map.75 = bf16[8,64,512]{2,1,0:T(8,128)(2,1)} custom-call(s32[8,16]{1,0:T(8,128)} %deal_ref.7, s32[128]{0:T(128)} %limit_ref.5, f32[1,128]{1,0:T(1,128)} %bitcast.7, f32[512,512]{1,0:T(8,128)} %get-tuple-element.40.own_ref, s16[528,512]{1,0:T(8,128)(2,1)} %copy-done.6), custom_call_target="tpu_custom_call" | custom-call | flops 5242880 | bytes 1048576 | tf_op jit(solution)/shard_map/pallas_call | solution.py:195
  45.9 6.1 %all-to-all-start.1 = ((bf16[8,64,512]{2,1,0:T(8,128)(2,1)}), bf16[8,64,512]{2,1,0:T(8,128)(2,1)S(1)}, u32[]{:S(2)}, u32[]{:S(2)}) async-start(bf16[8,64,512]{2,1,0:T(8,128)(2,1)} %shard_map.75), calls=%async_computation.1 | async-start | bytes 1048576 | tf_op jit(solution)/shard_map/all_to_all | solution.py:296
  52.0 0.0 collective-permute-done.2.refs_4_.refs_1_
  52.0 1.2 copy-done.2
  53.2 6.7 %shard_map.71 = s16[784,512]{1,0:T(8,128)(2,1)} custom-call(bf16[16,128,1024]{2,1,0:T(8,128)(2,1)} %bitcast.5, bf16[16,48,1024]{2,1,0:T(8,128)(2,1)} %copy-done.2, bf16[1024,512]{1,0:T(8,128)(2,1)} %get-tuple-element.23.refs_2_, bf16[1024,512]{1,0:T(8,128)(2,1)} %copy-done.3), custom_call_target="tpu_custom_call" | custom-call | flops 1610612736 | bytes 1605632 | tf_op jit(solution)/shard_map/pallas_call | solution.py:137
  59.9 1.5 %collective-permute-start.4 = (s16[784,512]{1,0:T(8,128)(2,1)}, s16[784,512]{1,0:T(8,128)(2,1)S(1)}, u32[]{:S(2)}, u32[]{:S(2)}) collective-permute-start(s16[784,512]{1,0:T(8,128)(2,1)} %shard_map.71), channel_id=1, source_target_pairs={{0,2},{1,3},{2,0},{3,1},{4,6},{5,7},{6,4},{7,5},{8,10},{9,11},{10,... | collective-permute-start | bytes 2408456 | tf_op jit(solution)/shard_map/ppermute | solution.py:266
  61.4 9.5 %shard_map.70 = (s16[784,512]{1,0:T(8,128)(2,1)}, f32[768,512]{1,0:T(8,128)}) custom-call(bf16[16,128,1024]{2,1,0:T(8,128)(2,1)} %bitcast.6, bf16[16,48,1024]{2,1,0:T(8,128)(2,1)} %collective-permute-done.refs_1_.refs_4_, bf16[1024,512]{1,0:T(8,128)(2,1)} %get-tuple-element.23.refs_2_, bf16[1024,512]{1,0:T(8,128)(2,1)} %copy-done.3, ...), custom_call_target="tpu_custom_call" | custom-call | flops 3221225472 | bytes 4751360 | tf_op jit(solution)/shard_map/pallas_call | solution.py:137
  70.9 8.0 %collective-permute-done.4.rest_0_ = s16[784,512]{1,0:T(8,128)(2,1)S(1)} collective-permute-done((s16[784,512]{1,0:T(8,128)(2,1)}, s16[784,512]{1,0:T(8,128)(2,1)S(1)}, u32[]{:S(2)}, u32[]{:S(2)}) %collective-permute-start.4) | collective-permute-done | bytes 802848 | tf_op jit(solution)/shard_map/ppermute | solution.py:266
  78.9 0.9 copy-done.5
  79.8 5.9 %shard_map.72 = bf16[8,96,512]{2,1,0:T(8,128)(2,1)} custom-call(s32[8,16]{1,0:T(8,128)} %deal_ref.7, s32[128]{0:T(128)} %limit_ref.5, f32[1,128]{1,0:T(1,128)} %bitcast.8, f32[768,512]{1,0:T(8,128)} %get-tuple-element.28.own_ref, s16[784,512]{1,0:T(8,128)(2,1)} %copy-done.5), custom_call_target="tpu_custom_call" | custom-call | flops 7864320 | bytes 1572864 | tf_op jit(solution)/shard_map/pallas_call | solution.py:195
  85.7 0.0 all-to-all-done.1.refs_9_
  85.7 6.0 %all-to-all-start = ((bf16[8,96,512]{2,1,0:T(8,128)(2,1)}), bf16[8,96,512]{2,1,0:T(8,128)(2,1)S(1)}, u32[]{:S(2)}, u32[]{:S(2)}) async-start(bf16[8,96,512]{2,1,0:T(8,128)(2,1)} %shard_map.72), calls=%async_computation | async-start | bytes 1572864 | tf_op jit(solution)/shard_map/all_to_all | solution.py:296
  91.7 1.5 %collective-permute-start.6 = (s16[784,512]{1,0:T(8,128)(2,1)}, s16[784,512]{1,0:T(8,128)(2,1)S(1)}, u32[]{:S(2)}, u32[]{:S(2)}) collective-permute-start(s16[784,512]{1,0:T(8,128)(2,1)} %get-tuple-element.31), channel_id=1, source_target_pairs={{0,2},{1,3},{2,0},{3,1},{4,6},{5,7},{6,4},{7,5},{8,10},{9,11},{10,... | collective-permute-start | bytes 2408456 | tf_op jit(solution)/shard_map/ppermute | solution.py:266
  93.2 16.1 %collective-permute-done.6.rest_0_ = s16[784,512]{1,0:T(8,128)(2,1)S(1)} collective-permute-done((s16[784,512]{1,0:T(8,128)(2,1)}, s16[784,512]{1,0:T(8,128)(2,1)S(1)}, u32[]{:S(2)}, u32[]{:S(2)}) %collective-permute-start.6) | collective-permute-done | bytes 802848 | tf_op jit(solution)/shard_map/ppermute | solution.py:266
  109.2 0.9 copy-done.4
  110.1 5.8 %shard_map.74 = (bf16[96,512]{1,0:T(8,128)(2,1)}, bf16[96,512]{1,0:T(8,128)(2,1)}, bf16[96,512]{1,0:T(8,128)(2,1)}, bf16[96,512]{1,0:T(8,128)(2,1)}, bf16[96,512...) custom-call(s32[8,16]{1,0:T(8,128)} %deal_ref.7, s32[128]{0:T(128)} %limit_ref.5, ...), custom_call_target="tpu_custom_call" | custom-call | flops 7864320 | bytes 1572864 | tf_op jit(solution)/shard_map/pallas_call | solution.py:195
  115.9 1.5 %collective-permute-start.7 = (bf16[96,512]{1,0:T(8,128)(2,1)}, bf16[96,512]{1,0:T(8,128)(2,1)S(1)}, u32[]{:S(2)}, u32[]{:S(2)}) collective-permute-start(bf16[96,512]{1,0:T(8,128)(2,1)} %get-tuple-element.33), channel_id=1, source_target_pairs={{0,4},{4,8},{8,12},{12,16},{16,20},{20,24},{24,28},{28,0},{1,5},{5... | collective-permute-start | bytes 294920 | tf_op jit(solution)/shard_map/ppermute | solution.py:300
  117.4 0.3 collective-permute-start.8
  117.7 1.7 %collective-permute-start.9 = (bf16[96,512]{1,0:T(8,128)(2,1)}, bf16[96,512]{1,0:T(8,128)(2,1)S(1)}, u32[]{:S(2)}, u32[]{:S(2)}) collective-permute-start(bf16[96,512]{1,0:T(8,128)(2,1)} %get-tuple-element.35), channel_id=1, source_target_pairs={{0,12},{4,16},{8,20},{12,24},{16,28},{20,0},{24,4},{28,8},{1,13},{... | collective-permute-start | bytes 294920 | tf_op jit(solution)/shard_map/ppermute | solution.py:300
  119.4 2.4 %collective-permute-start.10 = (bf16[96,512]{1,0:T(8,128)(2,1)}, bf16[96,512]{1,0:T(8,128)(2,1)S(1)}, u32[]{:S(2)}, u32[]{:S(2)}) collective-permute-start(bf16[96,512]{1,0:T(8,128)(2,1)} %get-tuple-element.36), channel_id=1, source_target_pairs={{0,16},{4,20},{8,24},{12,28},{16,0},{20,4},{24,8},{28,12},{1,17},{... | collective-permute-start | bytes 294920 | tf_op jit(solution)/shard_map/ppermute | solution.py:300
  121.8 1.5 %collective-permute-start.11 = (bf16[96,512]{1,0:T(8,128)(2,1)}, bf16[96,512]{1,0:T(8,128)(2,1)S(1)}, u32[]{:S(2)}, u32[]{:S(2)}) collective-permute-start(bf16[96,512]{1,0:T(8,128)(2,1)} %get-tuple-element.37), channel_id=1, source_target_pairs={{0,20},{4,24},{8,28},{12,0},{16,4},{20,8},{24,12},{28,16},{1,21},{... | collective-permute-start | bytes 294920 | tf_op jit(solution)/shard_map/ppermute | solution.py:300
  123.2 0.0 collective-permute-done.7.refs_2_
  123.3 0.6 collective-permute-start.12
  123.8 6.6 %collective-permute-done.8.refs_3_ = bf16[96,512]{1,0:T(8,128)(2,1)S(1)} collective-permute-done((bf16[96,512]{1,0:T(8,128)(2,1)}, bf16[96,512]{1,0:T(8,128)(2,1)S(1)}, u32[]{:S(2)}, u32[]{:S(2)}) %collective-permute-start.8) | collective-permute-done | bytes 98336 | tf_op jit(solution)/shard_map/ppermute | solution.py:300
  130.4 0.4 collective-permute-start.13
  130.9 1.7 %collective-permute-done.9.refs_4_ = bf16[96,512]{1,0:T(8,128)(2,1)S(1)} collective-permute-done((bf16[96,512]{1,0:T(8,128)(2,1)}, bf16[96,512]{1,0:T(8,128)(2,1)S(1)}, u32[]{:S(2)}, u32[]{:S(2)}) %collective-permute-start.9) | collective-permute-done | bytes 98336 | tf_op jit(solution)/shard_map/ppermute | solution.py:300
  132.5 0.0 collective-permute-done.10.refs_5_
  132.5 0.0 collective-permute-done.11.refs_6_
  132.5 0.0 collective-permute-done.12.refs_7_
  132.6 3.6 %collective-permute-done.13.refs_8_ = bf16[96,512]{1,0:T(8,128)(2,1)S(1)} collective-permute-done((bf16[96,512]{1,0:T(8,128)(2,1)}, bf16[96,512]{1,0:T(8,128)(2,1)S(1)}, u32[]{:S(2)}, u32[]{:S(2)}) %collective-permute-start.13) | collective-permute-done | bytes 98336 | tf_op jit(solution)/shard_map/ppermute | solution.py:300
  136.2 0.6 copy-done.13
  136.8 0.3 copy-done
  137.1 3.8 %shard_map.76 = (bf16[2048,256]{1,0:T(8,128)(2,1)}, bf16[2048,256]{1,0:T(8,128)(2,1)}) custom-call(s32[8,16]{1,0:T(8,128)} %deal_ref.7, bf16[8,96,512]{2,1,0:T(8,128)(2,1)} %copy-done, bf16[96,512]{1,0:T(8,128)(2,1)} %get-tuple-element.32.refs_1_, bf16[96,512]{1,0:T(8,128)(2,1)} %copy-done.7, bf16[96,512]{1,0:T(8,128)(2,1)} %copy-done.8, ...), custom_call_target="tpu_custom_call" | custom-call | flops 1000000 | bytes 4194304 | tf_op jit(solution)/shard_map/pallas_call | solution.py:235
  (23 shorter events, 0.0 us)
Async XLA Ops:
  5.3 10.3 %collective-permute-start = (bf16[16,48,1024]{2,1,0:T(8,128)(2,1)}, bf16[16,48,1024]{2,1,0:T(8,128)(2,1)}, u32[]{:S(2)}, u32[]{:S(2)}) collective-permute-start(bf16[16,48,1024]{2,1,0:T(8,128)(2,1)} %get-tuple-element.22), channel_id=1, source_target_pairs={{0,1},{1,0},{2,3},{3,2},{4,5},{5,4},{6,7},{7,6},{8,9},{9,8},{10,11... | collective-permute-start | bytes 4718600 | tf_op jit(solution)/shard_map/ppermute | solution.py:260
  9.4 3.0 %collective-permute-start.1 = (bf16[1024,512]{1,0:T(8,128)(2,1)}, bf16[1024,512]{1,0:T(8,128)(2,1)S(1)}, u32[]{:S(2)}, u32[]{:S(2)}) collective-permute-start(bf16[1024,512]{1,0:T(8,128)(2,1)} %get-tuple-element.24), channel_id=1, source_target_pairs={{0,1},{1,0},{2,3},{3,2},{4,5},{5,4},{6,7},{7,6},{8,9},{9,8},{10,11... | collective-permute-start | bytes 3145736 | tf_op jit(solution)/shard_map/ppermute | solution.py:260
  10.0 4.1 %collective-permute-start.3 = (bf16[1024,512]{1,0:T(8,128)(2,1)}, bf16[1024,512]{1,0:T(8,128)(2,1)}, u32[]{:S(2)}, u32[]{:S(2)}) collective-permute-start(bf16[1024,512]{1,0:T(8,128)(2,1)} %get-tuple-element.27), channel_id=1, source_target_pairs={{0,1},{1,0},{2,3},{3,2},{4,5},{5,4},{6,7},{7,6},{8,9},{9,8},{10,11... | collective-permute-start | bytes 3145736 | tf_op jit(solution)/shard_map/ppermute | solution.py:260
  10.0 5.5 %collective-permute-start.5 = (bf16[16,32,1024]{2,1,0:T(8,128)(2,1)}, bf16[16,32,1024]{2,1,0:T(8,128)(2,1)}, u32[]{:S(2)}, u32[]{:S(2)}) collective-permute-start(bf16[16,32,1024]{2,1,0:T(8,128)(2,1)} %get-tuple-element.29), channel_id=1, source_target_pairs={{0,1},{1,0},{2,3},{3,2},{4,5},{5,4},{6,7},{7,6},{8,9},{9,8},{10,11... | collective-permute-start | bytes 3145736 | tf_op jit(solution)/shard_map/ppermute | solution.py:260
  10.5 41.5 %collective-permute-start.2 = (bf16[16,48,1024]{2,1,0:T(8,128)(2,1)}, bf16[16,48,1024]{2,1,0:T(8,128)(2,1)S(1)}, u32[]{:S(2)}, u32[]{:S(2)}) collective-permute-start(bf16[16,48,1024]{2,1,0:T(8,128)(2,1)} %get-tuple-element.25), channel_id=1, source_target_pairs={{0,1},{1,0},{2,3},{3,2},{4,5},{5,4},{6,7},{7,6},{8,9},{9,8},{10,11... | collective-permute-start | bytes 4718600 | tf_op jit(solution)/shard_map/ppermute | solution.py:260
  12.5 3.1 %copy-start.3 = (bf16[1024,512]{1,0:T(8,128)(2,1)}, bf16[1024,512]{1,0:T(8,128)(2,1)S(1)}, u32[]{:S(2)}) copy-start(bf16[1024,512]{1,0:T(8,128)(2,1)S(1)} %collective-permute-done.1.refs_3_) | copy-start | bytes 3145732
  25.1 14.8 %collective-permute-start.14 = (s16[528,512]{1,0:T(8,128)(2,1)}, s16[528,512]{1,0:T(8,128)(2,1)S(1)}, u32[]{:S(2)}, u32[]{:S(2)}) collective-permute-start(s16[528,512]{1,0:T(8,128)(2,1)} %get-tuple-element.41), channel_id=1, source_target_pairs={{0,2},{1,3},{2,0},{3,1},{4,6},{5,7},{6,4},{7,5},{8,10},{9,11},{10,... | collective-permute-start | bytes 1622024 | tf_op jit(solution)/shard_map/ppermute | solution.py:266
  39.9 0.8 copy-start.6
  45.9 39.8 %all-to-all-start.1 = ((bf16[8,64,512]{2,1,0:T(8,128)(2,1)}), bf16[8,64,512]{2,1,0:T(8,128)(2,1)S(1)}, u32[]{:S(2)}, u32[]{:S(2)}) async-start(bf16[8,64,512]{2,1,0:T(8,128)(2,1)} %shard_map.75), calls=%async_computation.1 | async-start | bytes 1048576 | tf_op jit(solution)/shard_map/all_to_all | solution.py:296
  52.0 1.2 copy-start.2
  59.9 19.0 %collective-permute-start.4 = (s16[784,512]{1,0:T(8,128)(2,1)}, s16[784,512]{1,0:T(8,128)(2,1)S(1)}, u32[]{:S(2)}, u32[]{:S(2)}) collective-permute-start(s16[784,512]{1,0:T(8,128)(2,1)} %shard_map.71), channel_id=1, source_target_pairs={{0,2},{1,3},{2,0},{3,1},{4,6},{5,7},{6,4},{7,5},{8,10},{9,11},{10,... | collective-permute-start | bytes 2408456 | tf_op jit(solution)/shard_map/ppermute | solution.py:266
  78.9 0.9 copy-start.5
  85.7 30.2 %copy-start.1 = (bf16[8,64,512]{2,1,0:T(8,128)(2,1)}, bf16[8,64,512]{2,1,0:T(8,128)(2,1)S(1)}, u32[]{:S(2)}) copy-start(bf16[8,64,512]{2,1,0:T(8,128)(2,1)S(1)} %all-to-all-done.1.refs_9_) | copy-start | bytes 1572868
  85.7 50.5 %all-to-all-start = ((bf16[8,96,512]{2,1,0:T(8,128)(2,1)}), bf16[8,96,512]{2,1,0:T(8,128)(2,1)S(1)}, u32[]{:S(2)}, u32[]{:S(2)}) async-start(bf16[8,96,512]{2,1,0:T(8,128)(2,1)} %shard_map.72), calls=%async_computation | async-start | bytes 1572864 | tf_op jit(solution)/shard_map/all_to_all | solution.py:296
  91.7 17.6 %collective-permute-start.6 = (s16[784,512]{1,0:T(8,128)(2,1)}, s16[784,512]{1,0:T(8,128)(2,1)S(1)}, u32[]{:S(2)}, u32[]{:S(2)}) collective-permute-start(s16[784,512]{1,0:T(8,128)(2,1)} %get-tuple-element.31), channel_id=1, source_target_pairs={{0,2},{1,3},{2,0},{3,1},{4,6},{5,7},{6,4},{7,5},{8,10},{9,11},{10,... | collective-permute-start | bytes 2408456 | tf_op jit(solution)/shard_map/ppermute | solution.py:266
  109.2 0.9 copy-start.4
  115.9 7.3 %collective-permute-start.7 = (bf16[96,512]{1,0:T(8,128)(2,1)}, bf16[96,512]{1,0:T(8,128)(2,1)S(1)}, u32[]{:S(2)}, u32[]{:S(2)}) collective-permute-start(bf16[96,512]{1,0:T(8,128)(2,1)} %get-tuple-element.33), channel_id=1, source_target_pairs={{0,4},{4,8},{8,12},{12,16},{16,20},{20,24},{24,28},{28,0},{1,5},{5... | collective-permute-start | bytes 294920 | tf_op jit(solution)/shard_map/ppermute | solution.py:300
  117.4 13.0 %collective-permute-start.8 = (bf16[96,512]{1,0:T(8,128)(2,1)}, bf16[96,512]{1,0:T(8,128)(2,1)S(1)}, u32[]{:S(2)}, u32[]{:S(2)}) collective-permute-start(bf16[96,512]{1,0:T(8,128)(2,1)} %get-tuple-element.34), channel_id=1, source_target_pairs={{0,8},{4,12},{8,16},{12,20},{16,24},{20,28},{24,0},{28,4},{1,9},{5... | collective-permute-start | bytes 294920 | tf_op jit(solution)/shard_map/ppermute | solution.py:300
  117.7 14.8 %collective-permute-start.9 = (bf16[96,512]{1,0:T(8,128)(2,1)}, bf16[96,512]{1,0:T(8,128)(2,1)S(1)}, u32[]{:S(2)}, u32[]{:S(2)}) collective-permute-start(bf16[96,512]{1,0:T(8,128)(2,1)} %get-tuple-element.35), channel_id=1, source_target_pairs={{0,12},{4,16},{8,20},{12,24},{16,28},{20,0},{24,4},{28,8},{1,13},{... | collective-permute-start | bytes 294920 | tf_op jit(solution)/shard_map/ppermute | solution.py:300
  119.4 13.1 %collective-permute-start.10 = (bf16[96,512]{1,0:T(8,128)(2,1)}, bf16[96,512]{1,0:T(8,128)(2,1)S(1)}, u32[]{:S(2)}, u32[]{:S(2)}) collective-permute-start(bf16[96,512]{1,0:T(8,128)(2,1)} %get-tuple-element.36), channel_id=1, source_target_pairs={{0,16},{4,20},{8,24},{12,28},{16,0},{20,4},{24,8},{28,12},{1,17},{... | collective-permute-start | bytes 294920 | tf_op jit(solution)/shard_map/ppermute | solution.py:300
  121.8 10.7 %collective-permute-start.11 = (bf16[96,512]{1,0:T(8,128)(2,1)}, bf16[96,512]{1,0:T(8,128)(2,1)S(1)}, u32[]{:S(2)}, u32[]{:S(2)}) collective-permute-start(bf16[96,512]{1,0:T(8,128)(2,1)} %get-tuple-element.37), channel_id=1, source_target_pairs={{0,20},{4,24},{8,28},{12,0},{16,4},{20,8},{24,12},{28,16},{1,21},{... | collective-permute-start | bytes 294920 | tf_op jit(solution)/shard_map/ppermute | solution.py:300
  123.3 12.9 %copy-start.7 = (bf16[96,512]{1,0:T(8,128)(2,1)}, bf16[96,512]{1,0:T(8,128)(2,1)S(1)}, u32[]{:S(2)}) copy-start(bf16[96,512]{1,0:T(8,128)(2,1)S(1)} %collective-permute-done.7.refs_2_) | copy-start | bytes 294916
  123.3 9.3 %collective-permute-start.12 = (bf16[96,512]{1,0:T(8,128)(2,1)}, bf16[96,512]{1,0:T(8,128)(2,1)S(1)}, u32[]{:S(2)}, u32[]{:S(2)}) collective-permute-start(bf16[96,512]{1,0:T(8,128)(2,1)} %get-tuple-element.38), channel_id=1, source_target_pairs={{0,24},{4,28},{8,0},{12,4},{16,8},{20,12},{24,16},{28,20},{1,25},{... | collective-permute-start | bytes 294920 | tf_op jit(solution)/shard_map/ppermute | solution.py:300
  130.4 5.7 %copy-start.8 = (bf16[96,512]{1,0:T(8,128)(2,1)}, bf16[96,512]{1,0:T(8,128)(2,1)S(1)}, u32[]{:S(2)}) copy-start(bf16[96,512]{1,0:T(8,128)(2,1)S(1)} %collective-permute-done.8.refs_3_) | copy-start | bytes 294916
  130.4 5.7 %collective-permute-start.13 = (bf16[96,512]{1,0:T(8,128)(2,1)}, bf16[96,512]{1,0:T(8,128)(2,1)S(1)}, u32[]{:S(2)}, u32[]{:S(2)}) collective-permute-start(bf16[96,512]{1,0:T(8,128)(2,1)} %get-tuple-element.39), channel_id=1, source_target_pairs={{0,28},{4,0},{8,4},{12,8},{16,12},{20,16},{24,20},{28,24},{1,29},{... | collective-permute-start | bytes 294920 | tf_op jit(solution)/shard_map/ppermute | solution.py:300
  132.5 3.7 %copy-start.9 = (bf16[96,512]{1,0:T(8,128)(2,1)}, bf16[96,512]{1,0:T(8,128)(2,1)S(1)}, u32[]{:S(2)}) copy-start(bf16[96,512]{1,0:T(8,128)(2,1)S(1)} %collective-permute-done.9.refs_4_) | copy-start | bytes 294916
  132.5 3.7 %copy-start.10 = (bf16[96,512]{1,0:T(8,128)(2,1)}, bf16[96,512]{1,0:T(8,128)(2,1)S(1)}, u32[]{:S(2)}) copy-start(bf16[96,512]{1,0:T(8,128)(2,1)S(1)} %collective-permute-done.10.refs_5_) | copy-start | bytes 294916
  132.5 3.7 %copy-start.11 = (bf16[96,512]{1,0:T(8,128)(2,1)}, bf16[96,512]{1,0:T(8,128)(2,1)S(1)}, u32[]{:S(2)}) copy-start(bf16[96,512]{1,0:T(8,128)(2,1)S(1)} %collective-permute-done.11.refs_6_) | copy-start | bytes 294916
  132.5 3.7 %copy-start.12 = (bf16[96,512]{1,0:T(8,128)(2,1)}, bf16[96,512]{1,0:T(8,128)(2,1)S(1)}, u32[]{:S(2)}) copy-start(bf16[96,512]{1,0:T(8,128)(2,1)S(1)} %collective-permute-done.12.refs_7_) | copy-start | bytes 294916
  136.2 0.6 copy-start.13
  136.2 0.9 copy-start

commit v2 on v1

--- a/solution.py
+++ b/solution.py
@@ -21,9 +21,10 @@
 VMEM = pl.BlockSpec(memory_space=pltpu.VMEM)
 SMEM = pl.BlockSpec(memory_space=pltpu.SMEM)
 ANY = pl.BlockSpec(memory_space=pl.ANY)
-
-
-def call(body, ins, outs, shapes, flops, scratch=()):
+HBM = pl.BlockSpec(memory_space=pltpu.HBM)
+
+
+def call(body, ins, outs, shapes, flops, scratch=(), aliases={}):
     nbytes = sum(s.size * s.dtype.itemsize for s in shapes)
     return pl.pallas_call(
         body,
@@ -31,11 +32,13 @@
         out_specs=outs,
         out_shape=shapes,
         scratch_shapes=scratch,
+        input_output_aliases=aliases,
+        compiler_params=pltpu.CompilerParams(vmem_limit_bytes=16 * 2**20),
         cost_estimate=pl.CostEstimate(flops=int(flops), bytes_accessed=2 * nbytes, transcendentals=0),
     )
 
 
-STAGES = ((3, "a2a"), (3, "permute"), (2, "a2a"))
+STAGES = ((2, "permute"), (2, "a2a"), (2, "permute"), (2, "a2a"))
 
 
 def target(k):
@@ -59,7 +62,9 @@
     copies = []
     for i, k in enumerate(ks):
         for j, which in enumerate(target(k)):
-            w_out = weights[2 * i + j]
+            if k and j:
+                continue
+            w_out = weights[i] if not j else weights[len(ks)]
             for part in range(2):
                 start = pl.multiple_of((part * members + which) * share, share)
                 copies.append((w_ref.at[:, pl.ds(start, share)], w_out.at[:, part * share : (part + 1) * share]))
@@ -71,12 +76,12 @@
 def prepare(feats, w_kv, stages, ks, share):
     width = feats.shape[2]
     shapes = [jax.ShapeDtypeStruct((TPD, m, width), feats.dtype) for _, m in stages]
-    shapes += [jax.ShapeDtypeStruct((width, 2 * share), w_kv.dtype) for _ in range(2 * len(ks))]
+    shapes += [jax.ShapeDtypeStruct((width, 2 * share), w_kv.dtype) for _ in range(len(ks) + 1)]
     body = functools.partial(prepare_body, stages=stages, ks=ks, share=share)
     sems = [pltpu.SemaphoreType.DMA((len(stages) + 4 * len(ks),))]
-    got = call(body, [ANY, ANY], [VMEM] * len(shapes), shapes, 1e6, sems)(feats, w_kv)
+    got = call(body, [HBM, HBM], [VMEM] * len(shapes), shapes, 1e6, sems)(feats, w_kv)
     weights = got[len(stages) :]
-    return got[: len(stages)], weights[::2], weights[1::2]
+    return got[: len(stages)], weights[: len(ks)], weights[len(ks) :]
 
 
 def encode(total, out_ref, share):
@@ -143,23 +148,53 @@
     )(*inputs)
 
 
+def split(x, parts):
+    terms = []
+    for _ in range(parts):
+        term = x.astype(jnp.bfloat16)
+        terms.append(term)
+        x = x - term.astype(jnp.float32)
+    return jnp.concatenate(terms, axis=1)
+
+
 def finish_body(deal_ref, limit_ref, gain_ref, own_ref, *rest, stage, share, peers, span, mode):
     r0, m = stage
     rows = TPD * m
     groups = lax.axis_size("gx")
     own_index = lax.axis_index("gx")
-    codes, outs, scale_ref = rest[:peers], rest[peers:-1], rest[-1]
+    codes, outs, (saved_ref, done_ref) = rest[:peers], rest[peers:-2], rest[-2:]
     heads = 2 * share // HD
+    for p in range(peers):
+        saved_ref[p] = codes[p][rows : rows + PAD, :].astype(jnp.int32).astype(jnp.float32)
     line = lax.broadcasted_iota(jnp.int32, (HD, HD), 0)
-    for p in range(peers):
-        saved = codes[p][rows : rows + PAD, :].astype(jnp.int32).astype(jnp.float32)
-        for g in range(rows // HD):
+    at_head = lax.broadcasted_iota(jnp.int32, (3 * HD, 2 * share), 0) % HD
+    to_head = lax.broadcasted_iota(jnp.int32, (3 * HD, 2 * share), 1) // HD
+    spread = jnp.where(at_head == to_head, 1.0, 0.0).astype(jnp.bfloat16)
+    ones = jnp.ones((2 * HD, HD), jnp.bfloat16)
+    gain = gain_ref[...]
+
+    def block(g, carry):
+        at = pl.ds(pl.multiple_of(g * HD, HD), HD)
+        total = own_ref[at, :]
+        for p in range(peers):
+            saved = saved_ref[p, pl.ds(g, 1), :]
             stack = jnp.zeros((HD, HD), jnp.float32)
             for h in range(heads):
-                stack = jnp.where(line == h, saved[g : g + 1, h * HD : (h + 1) * HD], stack)
-            scale_ref[p, g * HD : (g + 1) * HD, :] = jnp.exp2(stack.T * (1.0 / STEPS)) * (1.0 / TOP)
-    gain = gain_ref[...]
-    position = r0 + lax.broadcasted_iota(jnp.int32, (m, HD), 0)
+                stack = jnp.where(line == h, saved[:, h * HD : (h + 1) * HD], stack)
+            scale = jnp.exp2(stack.T * (1.0 / STEPS)) * (1.0 / TOP)
+            wide = jnp.dot(split(scale, 3), spread, preferred_element_type=jnp.float32)
+            total += codes[p][at, :].astype(jnp.int32).astype(jnp.float32) * wide
+        for h in range(heads):
+            cols = slice(h * HD, (h + 1) * HD)
+            part = total[:, cols]
+            if h < heads // 2:
+                squares = jnp.dot(split(part * part, 2), ones, preferred_element_type=jnp.float32)
+                part = part * lax.rsqrt(squares * (1.0 / HD) + epsilon) * gain
+            done_ref[at, cols] = part
+        return carry
+
+    lax.fori_loop(0, rows // HD, block, 0, unroll=2)
+    position = r0 + lax.broadcasted_iota(jnp.int32, (m, 2 * share), 0)
     first = own_index * TPD
     for k in range(groups):
         taker = k if mode == "a2a" else (own_index + k) % groups
@@ -168,18 +203,9 @@
             tile = c * span
             for t in range(c * span, (c + 1) * span):
                 tile = jnp.where(deal_ref[taker, t] == first + t, t, tile)
-            inside = position < limit_ref[first + tile]
-            start = pl.multiple_of(tile * m, 16)
-            for h in range(heads):
-                cols = slice(h * HD, (h + 1) * HD)
-                total = own_ref[pl.ds(start, m), cols]
-                for p in range(peers):
-                    code = codes[p][pl.ds(start, m), cols].astype(jnp.int32).astype(jnp.float32)
-                    total += code * scale_ref[p, pl.ds(start, m), h : h + 1]
-                if h < heads // 2:
-                    mean_square = jnp.mean(total * total, axis=1, keepdims=True)
-                    total = total * lax.rsqrt(mean_square + epsilon) * gain
-                out[c * m : (c + 1) * m, cols] = jnp.where(inside, total, 0.0).astype(jnp.bfloat16)
+            kept = done_ref[pl.ds(pl.multiple_of(tile * m, 16), m), :]
+            kept = jnp.where(position < limit_ref[first + tile], kept, 0.0)
+            out[c * m : (c + 1) * m, :] = kept.astype(jnp.bfloat16)
 
 
 def finish(stage, deal, tile_rows, gain, own, codes, groups, share, span, mode):
@@ -198,14 +224,19 @@
         [VMEM] * len(shapes),
         shapes,
         40 * rows * share,
-        [pltpu.VMEM((max(1, len(codes)), rows, HD), jnp.float32)],
+        [
+            pltpu.VMEM((max(1, len(codes)), PAD, 2 * share), jnp.float32),
+            pltpu.VMEM((rows, 2 * share), jnp.float32),
+        ],
     )(deal, tile_rows, gain, own, *codes)
 
 
-def place_body(deal_ref, *refs, stages, modes, share, span):
+def place_body(deal_ref, *refs, stages, modes, share, span, held):
     groups = lax.axis_size("gx")
     own_index = lax.axis_index("gx")
     pieces, (keys_ref, values_ref, sem) = list(refs[:-3]), refs[-3:]
+    if held:
+        pieces = pieces[:-2]
     todo = []
     for s, ((r0, m), mode) in enumerate(zip(stages, modes)):
         whole = pieces.pop(0) if mode == "a2a" else None
@@ -230,16 +261,20 @@
         pl.when(slot >= 0)(copy.wait)
 
 
-def place(stages, modes, deal, pieces, groups, share, span):
+def place(stages, modes, deal, pieces, groups, share, span, before=()):
     shape = jax.ShapeDtypeStruct((TPD * TILE, share), jnp.bfloat16)
+    n = len(pieces)
     return call(
-        functools.partial(place_body, stages=stages, modes=modes, share=share, span=span),
-        [SMEM] + [VMEM] * len(pieces),
+        functools.partial(
+            place_body, stages=stages, modes=modes, share=share, span=span, held=bool(before)
+        ),
+        [SMEM] + [VMEM] * n + [ANY] * len(before),
         [ANY, ANY],
         [shape, shape],
         1e6,
         [pltpu.SemaphoreType.DMA((len(stages), groups, TPD // span, 2))],
-    )(deal, *pieces)
+        {n + 1: 0, n + 2: 1} if before else {},
+    )(deal, *pieces, *before)
 
 
 def local(image_feats, w_kv, k_gain, tile_rows, deal):
@@ -266,10 +301,18 @@
         return lax.ppermute(x, "gy", pairs)
 
     n = len(stages)
-    f0, w_far, w_send = prepare(feats, w_kv, stages[:1], range(1, chips), share)
+
+    def cut(which):
+        starts = (which * share, (members + which) * share)
+        parts = [lax.dynamic_slice(w_kv, (0, start), (w_kv.shape[0], share)) for start in starts]
+        return jnp.concatenate(parts, axis=1)
+
+    f0 = feats[:, stages[0][0] : sum(stages[0])]
+    w_send = [cut(target(k)[1]) for k in range(1, chips)]
+    near = [swap(f0)]
     v_far = [swap(w) for w in w_send]
-    near = [swap(f) for f in f0]
-    f1, (w_near,), w_send = prepare(feats, w_kv, stages[1:], (0,), share)
+    f1, w_own, w_send = prepare(feats, w_kv, stages[1:], range(chips), share)
+    w_near, w_far = w_own[0], w_own[1:]
     near += [swap(f) for f in f1]
     v_near = swap(w_send[0])
 
@@ -287,18 +330,20 @@
         if s:
             own[s - 1] = got[chips - 1]
             own[s] = got[-1]
-    pieces = []
+    pieces = [[] for _ in range(n)]
     for s in range(n):
         laid = finish(
             stages[s], deal, tile_rows, gain, own[s], codes[s], groups, share, span, modes[s]
         )
         if modes[s] == "a2a":
-            pieces.append(lax.all_to_all(laid[0], "gx", 0, 0, tiled=True))
+            pieces[s].append(lax.all_to_all(laid[0], "gx", 0, 0, tiled=True))
             continue
         for k, x in enumerate(laid):
             pairs = [(i, (i + k) % groups) for i in range(groups)]
-            pieces.append(lax.ppermute(x, "gx", pairs) if k else x)
-    return tuple(place(stages, modes, deal, pieces, groups, share, span))
+            pieces[s].append(lax.ppermute(x, "gx", pairs) if k else x)
+    early = n - 1
+    out = place(stages[:early], modes[:early], deal, sum(pieces[:early], []), groups, share, span)
+    return tuple(place(stages[early:], modes[early:], deal, sum(pieces[early:], []), groups, share, span, out))
 
 
 def solution(mesh):

time: 141 us -> 131 us (0.929)
  the two profiles are of different devices: /device:TPU:20 before, /device:TPU:0 now
where the time goes in v2:
time: 131 us
  waiting for transfers between devices  43.1 us (33%)
  starting transfers between devices  43 us (33%)
  Pallas kernels  27.8 us (21%)
  local copies, waits for them, and re-layouts  15.6 us (12%)
    ppermute x4, waiting for transfers between devices, along(): return lax.ppermute(x, 'gy', pairs)  33.8 us
    ppermute x14, starting transfers between devices, local(): pieces[s].append(lax.ppermute(x, 'gx', pairs) if k else x)  22.5 us
    unnamed x42, local copies, waits for them, and re-layouts  14.1 us
    pallas_call x4, Pallas kernels, project(): call(functools.partial(project_body, jobs=listed, share=share), [VMEM] *...  12.3 us
    all_to_all x2, starting transfers between devices, local(): pieces[s].append(lax.all_to_all(laid[0], 'gx', 0, 0, tiled=True))  11.8 us
    pallas_call x4, Pallas kernels, finish(): call(body, [SMEM, SMEM, VMEM, VMEM] + [VMEM] * len(codes), [VMEM] * len(s...  8.39 us
    ppermute x4, starting transfers between devices, along(): return lax.ppermute(x, 'gy', pairs)  6.48 us
    pallas_call x2, Pallas kernels, place(): call(functools.partial(place_body, stages=stages, modes=modes, share=shar...  5.36 us
  transfers between devices with their start and end apart: 26, of which 10 were waited for; matrix products, arithmetic and copies ran while one was open for 0% of the time, Pallas kernels for 20%

profile of v2, /device:TPU:0, one launch (start us, length us, event | category | flops | bytes accessed | tf_op | source)
XLA Modules:
  0.0 130.7 jit_solution(16990927417751122047)
XLA Ops:
  0.7 1.4 %constant_dynamic-slice_fusion.1 = (bf16[1024,256]{1,0:T(8,128)(2,1)S(1)}, bf16[1024,256]{1,0:T(8,128)(2,1)S(1)}) fusion(bf16[1024,2048]{1,0:T(8,128)(2,1)} %w_ref.1, s32[]{:T(128)S(6)} %select_n.24, s32[]{:T(128)S(6)} %select_n.25), kind=kLoop, calls=%fused_computation.2 | loop fusion | bytes 2097160 | tf_op jit(solution)/shard_map/dynamic_slice | solution.py:307
  3.2 2.2 %copy-done.3 = bf16[1024,2048]{1,0:T(8,128)(2,1)S(1)} copy-done((bf16[1024,2048]{1,0:T(8,128)(2,1)S(1)}, bf16[1024,2048]{1,0:T(8,128)(2,1)}, u32[]{:S(2)}) %copy-start.3) | copy-done | bytes 4194328
  5.4 1.7 %shard_map.68 = (bf16[16,32,1024]{2,1,0:T(8,128)(2,1)S(1)}, bf16[16,32,1024]{2,1,0:T(8,128)(2,1)S(1)}, bf16[16,32,1024]{2,1,0:T(8,128)(2,1)}, bf16[1024,512]{1,0...) custom-call(bf16[16,128,1024]{2,1,0:T(8,128)(2,1)S(1)} %bitcast.2, ...), custom_call_target="tpu_custom_call" | custom-call | flops 1000000 | bytes 12582912 | tf_op jit(solution)/shard_map/pallas_call | solution.py:82
  7.1 0.6 collective-permute-start.3
  8.9 1.1 collective-permute-done.3.refs_6_
  10.0 1.5 %collective-permute-done.5.refs_1_.refs_4_ = bf16[16,32,1024]{2,1,0:T(8,128)(2,1)S(1)} collective-permute-done((bf16[16,32,1024]{2,1,0:T(8,128)(2,1)S(1)}, bf16[16,32,1024]{2,1,0:T(8,128)(2,1)S(1)}, u32[]{:S(2)}, u32[]{:S(2)}) %collective-permute-start.5) | collective-permute-done | bytes 1048608 | tf_op jit(solution)/shard_map/ppermute | solution.py:295
  11.5 1.5 %collective-permute-done.6.refs_4_.refs_1_ = bf16[16,32,1024]{2,1,0:T(8,128)(2,1)S(1)} collective-permute-done((bf16[16,32,1024]{2,1,0:T(8,128)(2,1)S(1)}, bf16[16,32,1024]{2,1,0:T(8,128)(2,1)S(1)}, u32[]{:S(2)}, u32[]{:S(2)}) %collective-permute-start.6) | collective-permute-done | bytes 1048608 | tf_op jit(solution)/shard_map/ppermute | solution.py:295
  13.0 2.7 %shard_map.71 = (s16[528,512]{1,0:T(8,128)(2,1)S(1)}, f32[512,512]{1,0:T(8,128)S(1)}) custom-call(bf16[16,128,1024]{2,1,0:T(8,128)(2,1)S(1)} %bitcast.4, bf16[16,32,1024]{2,1,0:T(8,128)(2,1)S(1)} %collective-permute-done.5.refs_1_.refs_4_, bf16[1024,512]{1,0:T(8,128)(2,1)S(1)} %get-tuple-element.34.refs_2_, ...), custom_call_target="tpu_custom_call" | custom-call | flops 2147483648 | bytes 3178496 | tf_op jit(solution)/shard_map/pallas_call | solution.py:142
  15.8 2.9 %collective-permute-start.15 = (s16[528,512]{1,0:T(8,128)(2,1)S(1)}, s16[528,512]{1,0:T(8,128)(2,1)S(1)}, u32[]{:S(2)}, u32[]{:S(2)}) collective-permute-start(s16[528,512]{1,0:T(8,128)(2,1)S(1)} %get-tuple-element.51), channel_id=1, source_target_pairs={{0,2},{1,3},{2,0},{3,1},{4,6},{5,7},{6,4},{7,5},{8,10},{9,11},{10,... | collective-permute-start | bytes 1622024 | tf_op jit(solution)/shard_map/ppermute | solution.py:301
  18.7 2.7 %shard_map.74 = (s16[528,512]{1,0:T(8,128)(2,1)S(1)}, f32[512,512]{1,0:T(8,128)S(1)}) custom-call(bf16[16,128,1024]{2,1,0:T(8,128)(2,1)S(1)} %bitcast.5, bf16[16,32,1024]{2,1,0:T(8,128)(2,1)S(1)} %collective-permute-done.2.refs_4_.refs_1_, bf16[1024,512]{1,0:T(8,128)(2,1)S(1)} %get-tuple-element.34.refs_2_, ...), custom_call_target="tpu_custom_call" | custom-call | flops 2147483648 | bytes 3178496 | tf_op jit(solution)/shard_map/pallas_call | solution.py:142
  21.5 0.8 copy-done.19
  22.3 9.0 %collective-permute-done.15.rest_0_ = s16[528,512]{1,0:T(8,128)(2,1)S(1)} collective-permute-done((s16[528,512]{1,0:T(8,128)(2,1)S(1)}, s16[528,512]{1,0:T(8,128)(2,1)S(1)}, u32[]{:S(2)}, u32[]{:S(2)}) %collective-permute-start.15) | collective-permute-done | bytes 540704 | tf_op jit(solution)/shard_map/ppermute | solution.py:301
  31.3 2.1 %shard_map.75 = bf16[8,64,512]{2,1,0:T(8,128)(2,1)S(1)} custom-call(s32[8,16]{1,0:T(8,128)S(1)} %copy-done.16, s32[128]{0:T(128)S(1)} %copy-done.17, f32[1,128]{1,0:T(1,128)S(1)} %bitcast.8, f32[512,512]{1,0:T(8,128)S(1)} %get-tuple-element.50.own_ref, s16[528,512]{1,0:T(8,128)(2,1)S(1)} %collective-permute-done.15.rest_0_), custom_call_target="tpu_custom_call" | custom-call | flops 5242880 | bytes 1048576 | tf_op jit(solution)/shard_map/pallas_call | solution.py:221
  33.4 0.8 copy-done.9
  34.2 6.1 %all-to-all-start.1 = ((bf16[8,64,512]{2,1,0:T(8,128)(2,1)}), bf16[8,64,512]{2,1,0:T(8,128)(2,1)}, u32[]{:S(2)}, u32[]{:S(2)}) async-start(bf16[8,64,512]{2,1,0:T(8,128)(2,1)} %copy-done.9), calls=%async_computation.1 | async-start | bytes 1048576 | tf_op jit(solution)/shard_map/all_to_all | solution.py:339
  40.3 2.2 %copy-done.1 = bf16[2048,1024]{1,0:T(8,128)(2,1)S(1)} copy-done((bf16[2048,1024]{1,0:T(8,128)(2,1)S(1)}, bf16[2048,1024]{1,0:T(8,128)(2,1)}, u32[]{:S(2)}) %copy-start.1) | copy-done | bytes 4194328
  42.5 1.2 copy-done.5
  43.7 1.2 copy-done.7
  44.9 1.2 copy-done.11
  46.1 5.0 %shard_map.69 = (s16[528,512]{1,0:T(8,128)(2,1)S(1)}, f32[512,512]{1,0:T(8,128)S(1)}, f32[512,512]{1,0:T(8,128)S(1)}) custom-call(bf16[16,128,1024]{2,1,0:T(8,128)(2,1)S(1)} %bitcast.6, bf16[16,32,1024]{2,1,0:T(8,128)(2,1)} %collective-permute-done.refs_1_, bf16[1024,512]{1,0:T(8,128)(2,1)S(1)} %get-tuple-element.34.refs_2_, ...), custom_call_target="tpu_custom_call" | custom-call | flops 3221225472 | bytes 5275648 | tf_op jit(solution)/shard_map/pallas_call | solution.py:142
  51.2 1.0 copy-done.12
  52.1 1.5 %collective-permute-start.4 = (s16[528,512]{1,0:T(8,128)(2,1)S(1)}, s16[528,512]{1,0:T(8,128)(2,1)S(1)}, u32[]{:S(2)}, u32[]{:S(2)}) collective-permute-start(s16[528,512]{1,0:T(8,128)(2,1)S(1)} %get-tuple-element.39), channel_id=1, source_target_pairs={{0,2},{1,3},{2,0},{3,1},{4,6},{5,7},{6,4},{7,5},{8,10},{9,11},{10,... | collective-permute-start | bytes 1622024 | tf_op jit(solution)/shard_map/ppermute | solution.py:301
  53.6 11.7 %collective-permute-done.4.rest_0_ = s16[528,512]{1,0:T(8,128)(2,1)S(1)} collective-permute-done((s16[528,512]{1,0:T(8,128)(2,1)S(1)}, s16[528,512]{1,0:T(8,128)(2,1)S(1)}, u32[]{:S(2)}, u32[]{:S(2)}) %collective-permute-start.4) | collective-permute-done | bytes 540704 | tf_op jit(solution)/shard_map/ppermute | solution.py:301
  65.3 2.1 %shard_map.70 = bf16[8,64,512]{2,1,0:T(8,128)(2,1)S(1)} custom-call(s32[8,16]{1,0:T(8,128)S(1)} %copy-done.16, s32[128]{0:T(128)S(1)} %copy-done.17, f32[1,128]{1,0:T(1,128)S(1)} %bitcast.9, f32[512,512]{1,0:T(8,128)S(1)} %get-tuple-element.38.own_ref, s16[528,512]{1,0:T(8,128)(2,1)S(1)} %collective-permute-done.4.rest_0_), custom_call_target="tpu_custom_call" | custom-call | flops 5242880 | bytes 1048576 | tf_op jit(solution)/shard_map/pallas_call | solution.py:221
  67.4 0.8 copy-done.8
  68.2 5.7 %all-to-all-start = ((bf16[8,64,512]{2,1,0:T(8,128)(2,1)}), bf16[8,64,512]{2,1,0:T(8,128)(2,1)}, u32[]{:S(2)}, u32[]{:S(2)}) async-start(bf16[8,64,512]{2,1,0:T(8,128)(2,1)} %copy-done.8), calls=%async_computation | async-start | bytes 1048576 | tf_op jit(solution)/shard_map/all_to_all | solution.py:339
  73.9 2.2 %copy-done.2 = bf16[2048,1024]{1,0:T(8,128)(2,1)S(1)} copy-done((bf16[2048,1024]{1,0:T(8,128)(2,1)S(1)}, bf16[2048,1024]{1,0:T(8,128)(2,1)}, u32[]{:S(2)}) %copy-start.2) | copy-done | bytes 4194328
  76.1 1.8 %shard_map.72 = s16[528,512]{1,0:T(8,128)(2,1)S(1)} custom-call(bf16[16,128,1024]{2,1,0:T(8,128)(2,1)S(1)} %bitcast.7, bf16[16,32,1024]{2,1,0:T(8,128)(2,1)S(1)} %collective-permute-done.6.refs_4_.refs_1_, bf16[1024,512]{1,0:T(8,128)(2,1)S(1)} %get-tuple-element.34.refs_2_, bf16[1024,512]{1,0:T(8,128)(2,1)S(1)} %collective-permute-done.1.refs_3_), custom_call_target="tpu_custom_call" | custom-call | flops 1073741824 | bytes 1081344 | tf_op jit(solution)/shard_map/pallas_call | solution.py:142
  77.9 1.5 %collective-permute-start.7 = (s16[528,512]{1,0:T(8,128)(2,1)S(1)}, s16[528,512]{1,0:T(8,128)(2,1)S(1)}, u32[]{:S(2)}, u32[]{:S(2)}) collective-permute-start(s16[528,512]{1,0:T(8,128)(2,1)S(1)} %shard_map.72), channel_id=1, source_target_pairs={{0,2},{1,3},{2,0},{3,1},{4,6},{5,7},{6,4},{7,5},{8,10},{9,11},{10,... | collective-permute-start | bytes 1622024 | tf_op jit(solution)/shard_map/ppermute | solution.py:301
  80.0 13.1 %collective-permute-done.7.rest_0_ = s16[528,512]{1,0:T(8,128)(2,1)S(1)} collective-permute-done((s16[528,512]{1,0:T(8,128)(2,1)S(1)}, s16[528,512]{1,0:T(8,128)(2,1)S(1)}, u32[]{:S(2)}, u32[]{:S(2)}) %collective-permute-start.7) | collective-permute-done | bytes 540704 | tf_op jit(solution)/shard_map/ppermute | solution.py:301
  93.1 2.1 %shard_map.73 = (bf16[64,512]{1,0:T(8,128)(2,1)S(1)}, bf16[64,512]{1,0:T(8,128)(2,1)S(1)}, bf16[64,512]{1,0:T(8,128)(2,1)S(1)}, bf16[64,512]{1,0:T(8,128)(2,1)S(...) custom-call(s32[8,16]{1,0:T(8,128)S(1)} %copy-done.16, ...), custom_call_target="tpu_custom_call" | custom-call | flops 5242880 | bytes 1048576 | tf_op jit(solution)/shard_map/pallas_call | solution.py:221
  95.3 2.1 %collective-permute-start.8 = (bf16[64,512]{1,0:T(8,128)(2,1)S(1)}, bf16[64,512]{1,0:T(8,128)(2,1)S(1)}, u32[]{:S(2)}, u32[]{:S(2)}) collective-permute-start(bf16[64,512]{1,0:T(8,128)(2,1)S(1)} %get-tuple-element.43), channel_id=1, source_target_pairs={{0,4},{4,8},{8,12},{12,16},{16,20},{20,24},{24,28},{28,0},{1,5},{5... | collective-permute-start | bytes 196616 | tf_op jit(solution)/shard_map/ppermute | solution.py:343
  97.3 1.5 %collective-permute-start.9 = (bf16[64,512]{1,0:T(8,128)(2,1)S(1)}, bf16[64,512]{1,0:T(8,128)(2,1)S(1)}, u32[]{:S(2)}, u32[]{:S(2)}) collective-permute-start(bf16[64,512]{1,0:T(8,128)(2,1)S(1)} %get-tuple-element.44), channel_id=1, source_target_pairs={{0,8},{4,12},{8,16},{12,20},{16,24},{20,28},{24,0},{28,4},{1,9},{5... | collective-permute-start | bytes 196616 | tf_op jit(solution)/shard_map/ppermute | solution.py:343
  98.8 2.4 %collective-permute-start.10 = (bf16[64,512]{1,0:T(8,128)(2,1)S(1)}, bf16[64,512]{1,0:T(8,128)(2,1)S(1)}, u32[]{:S(2)}, u32[]{:S(2)}) collective-permute-start(bf16[64,512]{1,0:T(8,128)(2,1)S(1)} %get-tuple-element.45), channel_id=1, source_target_pairs={{0,12},{4,16},{8,20},{12,24},{16,28},{20,0},{24,4},{28,8},{1,13},{... | collective-permute-start | bytes 196616 | tf_op jit(solution)/shard_map/ppermute | solution.py:343
  101.2 1.5 %collective-permute-start.11 = (bf16[64,512]{1,0:T(8,128)(2,1)S(1)}, bf16[64,512]{1,0:T(8,128)(2,1)S(1)}, u32[]{:S(2)}, u32[]{:S(2)}) collective-permute-start(bf16[64,512]{1,0:T(8,128)(2,1)S(1)} %get-tuple-element.46), channel_id=1, source_target_pairs={{0,16},{4,20},{8,24},{12,28},{16,0},{20,4},{24,8},{28,12},{1,17},{... | collective-permute-start | bytes 196616 | tf_op jit(solution)/shard_map/ppermute | solution.py:343
  102.6 2.4 %collective-permute-start.12 = (bf16[64,512]{1,0:T(8,128)(2,1)S(1)}, bf16[64,512]{1,0:T(8,128)(2,1)S(1)}, u32[]{:S(2)}, u32[]{:S(2)}) collective-permute-start(bf16[64,512]{1,0:T(8,128)(2,1)S(1)} %get-tuple-element.47), channel_id=1, source_target_pairs={{0,20},{4,24},{8,28},{12,0},{16,4},{20,8},{24,12},{28,16},{1,21},{... | collective-permute-start | bytes 196616 | tf_op jit(solution)/shard_map/ppermute | solution.py:343
  105.0 2.1 %shard_map.76 = (bf16[64,512]{1,0:T(8,128)(2,1)S(1)}, bf16[64,512]{1,0:T(8,128)(2,1)S(1)}, bf16[64,512]{1,0:T(8,128)(2,1)S(1)}, bf16[64,512]{1,0:T(8,128)(2,1)S(...) custom-call(s32[8,16]{1,0:T(8,128)S(1)} %copy-done.16, ...), custom_call_target="tpu_custom_call" | custom-call | flops 5242880 | bytes 1048576 | tf_op jit(solution)/shard_map/pallas_call | solution.py:221
  107.1 1.5 %collective-permute-start.13 = (bf16[64,512]{1,0:T(8,128)(2,1)S(1)}, bf16[64,512]{1,0:T(8,128)(2,1)S(1)}, u32[]{:S(2)}, u32[]{:S(2)}) collective-permute-start(bf16[64,512]{1,0:T(8,128)(2,1)S(1)} %get-tuple-element.48), channel_id=1, source_target_pairs={{0,24},{4,28},{8,0},{12,4},{16,8},{20,12},{24,16},{28,20},{1,25},{... | collective-permute-start | bytes 196616 | tf_op jit(solution)/shard_map/ppermute | solution.py:343
  108.6 1.5 %collective-permute-start.14 = (bf16[64,512]{1,0:T(8,128)(2,1)S(1)}, bf16[64,512]{1,0:T(8,128)(2,1)S(1)}, u32[]{:S(2)}, u32[]{:S(2)}) collective-permute-start(bf16[64,512]{1,0:T(8,128)(2,1)S(1)} %get-tuple-element.49), channel_id=1, source_target_pairs={{0,28},{4,0},{8,4},{12,8},{16,12},{20,16},{24,20},{28,24},{1,29},{... | collective-permute-start | bytes 196616 | tf_op jit(solution)/shard_map/ppermute | solution.py:343
  110.7 0.6 collective-permute-start.18
  111.3 1.7 %collective-permute-start.19 = (bf16[64,512]{1,0:T(8,128)(2,1)S(1)}, bf16[64,512]{1,0:T(8,128)(2,1)S(1)}, u32[]{:S(2)}, u32[]{:S(2)}) collective-permute-start(bf16[64,512]{1,0:T(8,128)(2,1)S(1)} %get-tuple-element.57), channel_id=1, source_target_pairs={{0,12},{4,16},{8,20},{12,24},{16,28},{20,0},{24,4},{28,8},{1,13},{... | collective-permute-start | bytes 196616 | tf_op jit(solution)/shard_map/ppermute | solution.py:343
  113.0 3.0 %collective-permute-start.20 = (bf16[64,512]{1,0:T(8,128)(2,1)S(1)}, bf16[64,512]{1,0:T(8,128)(2,1)S(1)}, u32[]{:S(2)}, u32[]{:S(2)}) collective-permute-start(bf16[64,512]{1,0:T(8,128)(2,1)S(1)} %get-tuple-element.58), channel_id=1, source_target_pairs={{0,16},{4,20},{8,24},{12,28},{16,0},{20,4},{24,8},{28,12},{1,17},{... | collective-permute-start | bytes 196616 | tf_op jit(solution)/shard_map/ppermute | solution.py:343
  116.2 1.2 collective-permute-done.17.refs_10_
  117.4 3.5 %collective-permute-start.22 = (bf16[64,512]{1,0:T(8,128)(2,1)S(1)}, bf16[64,512]{1,0:T(8,128)(2,1)S(1)}, u32[]{:S(2)}, u32[]{:S(2)}) collective-permute-start(bf16[64,512]{1,0:T(8,128)(2,1)S(1)} %get-tuple-element.60), channel_id=1, source_target_pairs={{0,24},{4,28},{8,0},{12,4},{16,8},{20,12},{24,16},{28,20},{1,25},{... | collective-permute-start | bytes 196616 | tf_op jit(solution)/shard_map/ppermute | solution.py:343
  121.3 1.5 %collective-permute-done.22.refs_15_ = bf16[64,512]{1,0:T(8,128)(2,1)S(1)} collective-permute-done((bf16[64,512]{1,0:T(8,128)(2,1)S(1)}, bf16[64,512]{1,0:T(8,128)(2,1)S(1)}, u32[]{:S(2)}, u32[]{:S(2)}) %collective-permute-start.22) | collective-permute-done | bytes 65568 | tf_op jit(solution)/shard_map/ppermute | solution.py:343
  122.8 2.4 %collective-permute-done.23.refs_16_ = bf16[64,512]{1,0:T(8,128)(2,1)S(1)} collective-permute-done((bf16[64,512]{1,0:T(8,128)(2,1)S(1)}, bf16[64,512]{1,0:T(8,128)(2,1)S(1)}, u32[]{:S(2)}, u32[]{:S(2)}) %collective-permute-start.23) | collective-permute-done | bytes 65568 | tf_op jit(solution)/shard_map/ppermute | solution.py:343
  125.2 3.2 %shard_map.77 = (bf16[2048,256]{1,0:T(8,128)(2,1)}, bf16[2048,256]{1,0:T(8,128)(2,1)}) custom-call(s32[8,16]{1,0:T(8,128)S(1)} %copy-done.16, bf16[64,512]{1,0:T(8,128)(2,1)S(1)} %get-tuple-element.42.refs_0_, bf16[64,512]{1,0:T(8,128)(2,1)S(1)} %collective-permute-done.8.refs_1_, bf16[64,512]{1,0:T(8,128)(2,1)S(1)} %collective-permute-done.9.refs_2_, ...), custom_call_target="tpu_custom_call" | custom-call | flops 1000000 | bytes 4194304 | tf_op jit(solution)/shard_map/pallas_call | solution.py:267
  128.3 2.2 %shard_map.78 = (bf16[2048,256]{1,0:T(8,128)(2,1)}, bf16[2048,256]{1,0:T(8,128)(2,1)}) custom-call(s32[8,16]{1,0:T(8,128)S(1)} %copy-done.16, bf16[8,64,512]{2,1,0:T(8,128)(2,1)} %all-to-all-done.refs_0_, bf16[2048,256]{1,0:T(8,128)(2,1)} %get-tuple-element.62.refs_1_, ...), custom_call_target="tpu_custom_call", output_to_operand_aliasing={{0}: (2, {}), {1}: (3, {})} | custom-call | flops 1000000 | bytes 4194304 | tf_op jit(solution)/shard_map/pallas_call | solution.py:267
  (60 shorter events, 4.1 us)
Async XLA Ops:
  0.7 2.5 %copy-start = (bf16[2048,1024]{1,0:T(8,128)(2,1)S(1)}, bf16[2048,1024]{1,0:T(8,128)(2,1)}, u32[]{:S(2)}) copy-start(bf16[2048,1024]{1,0:T(8,128)(2,1)} %param.5) | copy-start | bytes 12582916
  2.2 6.3 %collective-permute-start.1 = (bf16[1024,512]{1,0:T(8,128)(2,1)S(1)}, bf16[1024,512]{1,0:T(8,128)(2,1)S(1)}, u32[]{:S(2)}, u32[]{:S(2)}) collective-permute-start(bf16[1024,512]{1,0:T(8,128)(2,1)S(1)} %pad_maximum_fusion), channel_id=1, source_target_pairs={{0,1},{1,0},{2,3},{3,2},{4,5},{5,4},{6,7},{7,6},{8,9},{9,8},{10,11... | collective-permute-start | bytes 3145736 | tf_op jit(solution)/shard_map/ppermute | solution.py:295
  3.2 2.2 %copy-start.3 = (bf16[1024,2048]{1,0:T(8,128)(2,1)S(1)}, bf16[1024,2048]{1,0:T(8,128)(2,1)}, u32[]{:S(2)}) copy-start(bf16[1024,2048]{1,0:T(8,128)(2,1)} %w_ref.1) | copy-start | bytes 12582916
  7.1 11.6 %copy-start.4 = (bf16[1024,512]{1,0:T(8,128)(2,1)}, bf16[1024,512]{1,0:T(8,128)(2,1)S(1)}, u32[]{:S(2)}) copy-start(bf16[1024,512]{1,0:T(8,128)(2,1)S(1)} %get-tuple-element.36.refs_5_) | copy-start | bytes 3145732
  7.1 2.8 %collective-permute-start.3 = (bf16[1024,512]{1,0:T(8,128)(2,1)S(1)}, bf16[1024,512]{1,0:T(8,128)(2,1)S(1)}, u32[]{:S(2)}, u32[]{:S(2)}) collective-permute-start(bf16[1024,512]{1,0:T(8,128)(2,1)S(1)} %get-tuple-element.37), channel_id=1, source_target_pairs={{0,1},{1,0},{2,3},{3,2},{4,5},{5,4},{6,7},{7,6},{8,9},{9,8},{10,11... | collective-permute-start | bytes 3145736 | tf_op jit(solution)/shard_map/ppermute | solution.py:295
  7.7 3.8 %collective-permute-start.5 = (bf16[16,32,1024]{2,1,0:T(8,128)(2,1)S(1)}, bf16[16,32,1024]{2,1,0:T(8,128)(2,1)S(1)}, u32[]{:S(2)}, u32[]{:S(2)}) collective-permute-start(bf16[16,32,1024]{2,1,0:T(8,128)(2,1)S(1)} %get-tuple-element.40), channel_id=1, source_target_pairs={{0,1},{1,0},{2,3},{3,2},{4,5},{5,4},{6,7},{7,6},{8,9},{9,8},{10,11... | collective-permute-start | bytes 3145736 | tf_op jit(solution)/shard_map/ppermute | solution.py:295
  7.9 5.1 %collective-permute-start.6 = (bf16[16,32,1024]{2,1,0:T(8,128)(2,1)S(1)}, bf16[16,32,1024]{2,1,0:T(8,128)(2,1)S(1)}, u32[]{:S(2)}, u32[]{:S(2)}) collective-permute-start(bf16[16,32,1024]{2,1,0:T(8,128)(2,1)S(1)} %slice.4), channel_id=1, source_target_pairs={{0,1},{1,0},{2,3},{3,2},{4,5},{5,4},{6,7},{7,6},{8,9},{9,8},{10,11... | collective-permute-start | bytes 3145736 | tf_op jit(solution)/shard_map/ppermute | solution.py:295
  8.4 10.3 %collective-permute-start.2 = (bf16[16,32,1024]{2,1,0:T(8,128)(2,1)S(1)}, bf16[16,32,1024]{2,1,0:T(8,128)(2,1)S(1)}, u32[]{:S(2)}, u32[]{:S(2)}) collective-permute-start(bf16[16,32,1024]{2,1,0:T(8,128)(2,1)S(1)} %get-tuple-element.35), channel_id=1, source_target_pairs={{0,1},{1,0},{2,3},{3,2},{4,5},{5,4},{6,7},{7,6},{8,9},{9,8},{10,11... | collective-permute-start | bytes 3145736 | tf_op jit(solution)/shard_map/ppermute | solution.py:295
  8.5 31.8 %collective-permute-start = (bf16[16,32,1024]{2,1,0:T(8,128)(2,1)}, bf16[16,32,1024]{2,1,0:T(8,128)(2,1)}, u32[]{:S(2)}, u32[]{:S(2)}) collective-permute-start(bf16[16,32,1024]{2,1,0:T(8,128)(2,1)} %get-tuple-element.33), channel_id=1, source_target_pairs={{0,1},{1,0},{2,3},{3,2},{4,5},{5,4},{6,7},{7,6},{8,9},{9,8},{10,11... | collective-permute-start | bytes 3145736 | tf_op jit(solution)/shard_map/ppermute | solution.py:295
  10.0 8.7 %copy-start.6 = (bf16[1024,512]{1,0:T(8,128)(2,1)}, bf16[1024,512]{1,0:T(8,128)(2,1)S(1)}, u32[]{:S(2)}) copy-start(bf16[1024,512]{1,0:T(8,128)(2,1)S(1)} %collective-permute-done.3.refs_6_) | copy-start | bytes 3145732
  15.7 5.7 %copy-start.14 = (f32[512,512]{1,0:T(8,128)}, f32[512,512]{1,0:T(8,128)S(1)}, u32[]{:S(2)}) copy-start(f32[512,512]{1,0:T(8,128)S(1)} %get-tuple-element.41.own_ref) | copy-start | bytes 3145732
  15.7 15.5 %copy-start.16 = (s32[8,16]{1,0:T(8,128)S(1)}, s32[8,16]{1,0:T(8,128)}, u32[]{:S(2)}) copy-start(s32[8,16]{1,0:T(8,128)} %deal_ref.11) | copy-start | bytes 1540
  15.8 15.5 %copy-start.17 = (s32[128]{0:T(128)S(1)}, s32[128]{0:T(128)}, u32[]{:S(2)}) copy-start(s32[128]{0:T(128)} %limit_ref.7) | copy-start | bytes 1540
  15.8 15.5 %copy-start.18 = (f32[128]{0:T(128)S(1)}, f32[128]{0:T(128)}, u32[]{:S(2)}) copy-start(f32[128]{0:T(128)} %param.7) | copy-start | bytes 1540
  15.8 15.5 %collective-permute-start.15 = (s16[528,512]{1,0:T(8,128)(2,1)S(1)}, s16[528,512]{1,0:T(8,128)(2,1)S(1)}, u32[]{:S(2)}, u32[]{:S(2)}) collective-permute-start(s16[528,512]{1,0:T(8,128)(2,1)S(1)} %get-tuple-element.51), channel_id=1, source_target_pairs={{0,2},{1,3},{2,0},{3,1},{4,6},{5,7},{6,4},{7,5},{8,10},{9,11},{10,... | collective-permute-start | bytes 1622024 | tf_op jit(solution)/shard_map/ppermute | solution.py:301
  18.7 2.8 %copy-start.10 = (bf16[16,32,1024]{2,1,0:T(8,128)(2,1)}, bf16[16,32,1024]{2,1,0:T(8,128)(2,1)S(1)}, u32[]{:S(2)}) copy-start(bf16[16,32,1024]{2,1,0:T(8,128)(2,1)S(1)} %collective-permute-done.2.refs_4_.refs_1_) | copy-start | bytes 3145732
  21.5 0.8 copy-start.19
  33.4 0.8 copy-start.9
  34.2 34.0 %all-to-all-start.1 = ((bf16[8,64,512]{2,1,0:T(8,128)(2,1)}), bf16[8,64,512]{2,1,0:T(8,128)(2,1)}, u32[]{:S(2)}, u32[]{:S(2)}) async-start(bf16[8,64,512]{2,1,0:T(8,128)(2,1)} %copy-done.9), calls=%async_computation.1 | async-start | bytes 1048576 | tf_op jit(solution)/shard_map/all_to_all | solution.py:339
  40.3 2.2 %copy-start.1 = (bf16[2048,1024]{1,0:T(8,128)(2,1)S(1)}, bf16[2048,1024]{1,0:T(8,128)(2,1)}, u32[]{:S(2)}) copy-start(bf16[2048,1024]{1,0:T(8,128)(2,1)} %param.5) | copy-start | bytes 12582916
  42.5 1.2 copy-start.5
  43.7 1.2 copy-start.7
  44.9 1.2 copy-start.11
  51.2 1.0 copy-start.12
  52.1 13.2 %collective-permute-start.4 = (s16[528,512]{1,0:T(8,128)(2,1)S(1)}, s16[528,512]{1,0:T(8,128)(2,1)S(1)}, u32[]{:S(2)}, u32[]{:S(2)}) collective-permute-start(s16[528,512]{1,0:T(8,128)(2,1)S(1)} %get-tuple-element.39), channel_id=1, source_target_pairs={{0,2},{1,3},{2,0},{3,1},{4,6},{5,7},{6,4},{7,5},{8,10},{9,11},{10,... | collective-permute-start | bytes 1622024 | tf_op jit(solution)/shard_map/ppermute | solution.py:301
  67.4 0.8 copy-start.8
  68.2 60.1 %all-to-all-start = ((bf16[8,64,512]{2,1,0:T(8,128)(2,1)}), bf16[8,64,512]{2,1,0:T(8,128)(2,1)}, u32[]{:S(2)}, u32[]{:S(2)}) async-start(bf16[8,64,512]{2,1,0:T(8,128)(2,1)} %copy-done.8), calls=%async_computation | async-start | bytes 1048576 | tf_op jit(solution)/shard_map/all_to_all | solution.py:339
  73.9 2.2 %copy-start.2 = (bf16[2048,1024]{1,0:T(8,128)(2,1)S(1)}, bf16[2048,1024]{1,0:T(8,128)(2,1)}, u32[]{:S(2)}) copy-start(bf16[2048,1024]{1,0:T(8,128)(2,1)} %param.5) | copy-start | bytes 12582916
  76.1 3.3 %copy-start.20 = (s16[528,512]{1,0:T(8,128)(2,1)S(1)}, s16[528,512]{1,0:T(8,128)(2,1)}, u32[]{:S(2)}) copy-start(s16[528,512]{1,0:T(8,128)(2,1)} %copy-done.19) | copy-start | bytes 1622020
  76.1 17.0 %copy-start.15 = (f32[512,512]{1,0:T(8,128)S(1)}, f32[512,512]{1,0:T(8,128)}, u32[]{:S(2)}) copy-start(f32[512,512]{1,0:T(8,128)} %copy-done.14) | copy-start | bytes 3145732
  76.1 28.9 %copy-start.13 = (f32[512,512]{1,0:T(8,128)S(1)}, f32[512,512]{1,0:T(8,128)}, u32[]{:S(2)}) copy-start(f32[512,512]{1,0:T(8,128)} %copy-done.12) | copy-start | bytes 3145732
  77.9 15.2 %collective-permute-start.7 = (s16[528,512]{1,0:T(8,128)(2,1)S(1)}, s16[528,512]{1,0:T(8,128)(2,1)S(1)}, u32[]{:S(2)}, u32[]{:S(2)}) collective-permute-start(s16[528,512]{1,0:T(8,128)(2,1)S(1)} %shard_map.72), channel_id=1, source_target_pairs={{0,2},{1,3},{2,0},{3,1},{4,6},{5,7},{6,4},{7,5},{8,10},{9,11},{10,... | collective-permute-start | bytes 1622024 | tf_op jit(solution)/shard_map/ppermute | solution.py:301
  79.5 23.2 %collective-permute-start.16 = (s16[528,512]{1,0:T(8,128)(2,1)S(1)}, s16[528,512]{1,0:T(8,128)(2,1)S(1)}, u32[]{:S(2)}, u32[]{:S(2)}) collective-permute-start(s16[528,512]{1,0:T(8,128)(2,1)S(1)} %copy-done.20), channel_id=1, source_target_pairs={{0,2},{1,3},{2,0},{3,1},{4,6},{5,7},{6,4},{7,5},{8,10},{9,11},{10,... | collective-permute-start | bytes 1622024 | tf_op jit(solution)/shard_map/ppermute | solution.py:301
  95.3 11.9 %collective-permute-start.8 = (bf16[64,512]{1,0:T(8,128)(2,1)S(1)}, bf16[64,512]{1,0:T(8,128)(2,1)S(1)}, u32[]{:S(2)}, u32[]{:S(2)}) collective-permute-start(bf16[64,512]{1,0:T(8,128)(2,1)S(1)} %get-tuple-element.43), channel_id=1, source_target_pairs={{0,4},{4,8},{8,12},{12,16},{16,20},{20,24},{24,28},{28,0},{1,5},{5... | collective-permute-start | bytes 196616 | tf_op jit(solution)/shard_map/ppermute | solution.py:343
  97.3 11.3 %collective-permute-start.9 = (bf16[64,512]{1,0:T(8,128)(2,1)S(1)}, bf16[64,512]{1,0:T(8,128)(2,1)S(1)}, u32[]{:S(2)}, u32[]{:S(2)}) collective-permute-start(bf16[64,512]{1,0:T(8,128)(2,1)S(1)} %get-tuple-element.44), channel_id=1, source_target_pairs={{0,8},{4,12},{8,16},{12,20},{16,24},{20,28},{24,0},{28,4},{1,9},{5... | collective-permute-start | bytes 196616 | tf_op jit(solution)/shard_map/ppermute | solution.py:343
  98.8 11.3 %collective-permute-start.10 = (bf16[64,512]{1,0:T(8,128)(2,1)S(1)}, bf16[64,512]{1,0:T(8,128)(2,1)S(1)}, u32[]{:S(2)}, u32[]{:S(2)}) collective-permute-start(bf16[64,512]{1,0:T(8,128)(2,1)S(1)} %get-tuple-element.45), channel_id=1, source_target_pairs={{0,12},{4,16},{8,20},{12,24},{16,28},{20,0},{24,4},{28,8},{1,13},{... | collective-permute-start | bytes 196616 | tf_op jit(solution)/shard_map/ppermute | solution.py:343
  101.2 9.5 %collective-permute-start.11 = (bf16[64,512]{1,0:T(8,128)(2,1)S(1)}, bf16[64,512]{1,0:T(8,128)(2,1)S(1)}, u32[]{:S(2)}, u32[]{:S(2)}) collective-permute-start(bf16[64,512]{1,0:T(8,128)(2,1)S(1)} %get-tuple-element.46), channel_id=1, source_target_pairs={{0,16},{4,20},{8,24},{12,28},{16,0},{20,4},{24,8},{28,12},{1,17},{... | collective-permute-start | bytes 196616 | tf_op jit(solution)/shard_map/ppermute | solution.py:343
  102.6 8.6 %collective-permute-start.12 = (bf16[64,512]{1,0:T(8,128)(2,1)S(1)}, bf16[64,512]{1,0:T(8,128)(2,1)S(1)}, u32[]{:S(2)}, u32[]{:S(2)}) collective-permute-start(bf16[64,512]{1,0:T(8,128)(2,1)S(1)} %get-tuple-element.47), channel_id=1, source_target_pairs={{0,20},{4,24},{8,28},{12,0},{16,4},{20,8},{24,12},{28,16},{1,21},{... | collective-permute-start | bytes 196616 | tf_op jit(solution)/shard_map/ppermute | solution.py:343
  107.1 5.9 %collective-permute-start.13 = (bf16[64,512]{1,0:T(8,128)(2,1)S(1)}, bf16[64,512]{1,0:T(8,128)(2,1)S(1)}, u32[]{:S(2)}, u32[]{:S(2)}) collective-permute-start(bf16[64,512]{1,0:T(8,128)(2,1)S(1)} %get-tuple-element.48), channel_id=1, source_target_pairs={{0,24},{4,28},{8,0},{12,4},{16,8},{20,12},{24,16},{28,20},{1,25},{... | collective-permute-start | bytes 196616 | tf_op jit(solution)/shard_map/ppermute | solution.py:343
  108.6 7.3 %collective-permute-start.14 = (bf16[64,512]{1,0:T(8,128)(2,1)S(1)}, bf16[64,512]{1,0:T(8,128)(2,1)S(1)}, u32[]{:S(2)}, u32[]{:S(2)}) collective-permute-start(bf16[64,512]{1,0:T(8,128)(2,1)S(1)} %get-tuple-element.49), channel_id=1, source_target_pairs={{0,28},{4,0},{8,4},{12,8},{16,12},{20,16},{24,20},{28,24},{1,29},{... | collective-permute-start | bytes 196616 | tf_op jit(solution)/shard_map/ppermute | solution.py:343
  110.1 7.2 %collective-permute-start.17 = (bf16[64,512]{1,0:T(8,128)(2,1)S(1)}, bf16[64,512]{1,0:T(8,128)(2,1)S(1)}, u32[]{:S(2)}, u32[]{:S(2)}) collective-permute-start(bf16[64,512]{1,0:T(8,128)(2,1)S(1)} %get-tuple-element.55), channel_id=1, source_target_pairs={{0,4},{4,8},{8,12},{12,16},{16,20},{20,24},{24,28},{28,0},{1,5},{5... | collective-permute-start | bytes 196616 | tf_op jit(solution)/shard_map/ppermute | solution.py:343
  110.7 10.2 %collective-permute-start.18 = (bf16[64,512]{1,0:T(8,128)(2,1)S(1)}, bf16[64,512]{1,0:T(8,128)(2,1)S(1)}, u32[]{:S(2)}, u32[]{:S(2)}) collective-permute-start(bf16[64,512]{1,0:T(8,128)(2,1)S(1)} %get-tuple-element.56), channel_id=1, source_target_pairs={{0,8},{4,12},{8,16},{12,20},{16,24},{20,28},{24,0},{28,4},{1,9},{5... | collective-permute-start | bytes 196616 | tf_op jit(solution)/shard_map/ppermute | solution.py:343
  111.3 9.9 %collective-permute-start.19 = (bf16[64,512]{1,0:T(8,128)(2,1)S(1)}, bf16[64,512]{1,0:T(8,128)(2,1)S(1)}, u32[]{:S(2)}, u32[]{:S(2)}) collective-permute-start(bf16[64,512]{1,0:T(8,128)(2,1)S(1)} %get-tuple-element.57), channel_id=1, source_target_pairs={{0,12},{4,16},{8,20},{12,24},{16,28},{20,0},{24,4},{28,8},{1,13},{... | collective-permute-start | bytes 196616 | tf_op jit(solution)/shard_map/ppermute | solution.py:343
  113.0 8.2 %collective-permute-start.20 = (bf16[64,512]{1,0:T(8,128)(2,1)S(1)}, bf16[64,512]{1,0:T(8,128)(2,1)S(1)}, u32[]{:S(2)}, u32[]{:S(2)}) collective-permute-start(bf16[64,512]{1,0:T(8,128)(2,1)S(1)} %get-tuple-element.58), channel_id=1, source_target_pairs={{0,16},{4,20},{8,24},{12,28},{16,0},{20,4},{24,8},{28,12},{1,17},{... | collective-permute-start | bytes 196616 | tf_op jit(solution)/shard_map/ppermute | solution.py:343
  116.0 5.3 %collective-permute-start.21 = (bf16[64,512]{1,0:T(8,128)(2,1)S(1)}, bf16[64,512]{1,0:T(8,128)(2,1)S(1)}, u32[]{:S(2)}, u32[]{:S(2)}) collective-permute-start(bf16[64,512]{1,0:T(8,128)(2,1)S(1)} %get-tuple-element.59), channel_id=1, source_target_pairs={{0,20},{4,24},{8,28},{12,0},{16,4},{20,8},{24,12},{28,16},{1,21},{... | collective-permute-start | bytes 196616 | tf_op jit(solution)/shard_map/ppermute | solution.py:343
  117.4 5.4 %collective-permute-start.22 = (bf16[64,512]{1,0:T(8,128)(2,1)S(1)}, bf16[64,512]{1,0:T(8,128)(2,1)S(1)}, u32[]{:S(2)}, u32[]{:S(2)}) collective-permute-start(bf16[64,512]{1,0:T(8,128)(2,1)S(1)} %get-tuple-element.60), channel_id=1, source_target_pairs={{0,24},{4,28},{8,0},{12,4},{16,8},{20,12},{24,16},{28,20},{1,25},{... | collective-permute-start | bytes 196616 | tf_op jit(solution)/shard_map/ppermute | solution.py:343
  120.9 4.3 %collective-permute-start.23 = (bf16[64,512]{1,0:T(8,128)(2,1)S(1)}, bf16[64,512]{1,0:T(8,128)(2,1)S(1)}, u32[]{:S(2)}, u32[]{:S(2)}) collective-permute-start(bf16[64,512]{1,0:T(8,128)(2,1)S(1)} %get-tuple-element.61), channel_id=1, source_target_pairs={{0,28},{4,0},{8,4},{12,8},{16,12},{20,16},{24,20},{28,24},{1,29},{... | collective-permute-start | bytes 196616 | tf_op jit(solution)/shard_map/ppermute | solution.py:343

commit v3 on v2

--- a/solution.py
+++ b/solution.py
@@ -33,7 +33,7 @@
         out_shape=shapes,
         scratch_shapes=scratch,
         input_output_aliases=aliases,
-        compiler_params=pltpu.CompilerParams(vmem_limit_bytes=16 * 2**20),
+        compiler_params=pltpu.CompilerParams(vmem_limit_bytes=8 * 2**20),
         cost_estimate=pl.CostEstimate(flops=int(flops), bytes_accessed=2 * nbytes, transcendentals=0),
     )
 
@@ -193,7 +193,7 @@
             done_ref[at, cols] = part
         return carry
 
-    lax.fori_loop(0, rows // HD, block, 0, unroll=2)
+    lax.fori_loop(0, rows // HD, block, 0, unroll=4)
     position = r0 + lax.broadcasted_iota(jnp.int32, (m, 2 * share), 0)
     first = own_index * TPD
     for k in range(groups):
@@ -201,8 +201,8 @@
         out = outs[0].at[k] if mode == "a2a" else outs[k]
         for c in range(TPD // span):
             tile = c * span
-            for t in range(c * span, (c + 1) * span):
-                tile = jnp.where(deal_ref[taker, t] == first + t, t, tile)
+            for t in range(c * span + 1, (c + 1) * span):
+                tile += jnp.where(deal_ref[taker, t] == first + t, t - c * span, 0)
             kept = done_ref[pl.ds(pl.multiple_of(tile * m, 16), m), :]
             kept = jnp.where(position < limit_ref[first + tile], kept, 0.0)
             out[c * m : (c + 1) * m, :] = kept.astype(jnp.bfloat16)

time: 131 us -> 131 us (level)
  transfers between devices with their start and end apart: 26 -> 26, of which waited for: 10 -> 9; matrix products, arithmetic and copies ran while one was open for 0% -> 0% of each run, Pallas kernels for 20% -> 19%
where the time goes in v3:
time: 131 us; the launch traced here: 130 us
  starting transfers between devices  43.2 us (33%)
  waiting for transfers between devices  43.2 us (33%)
  Pallas kernels  26.8 us (20%)
  local copies, waits for them, and re-layouts  15.6 us (12%)
    ppermute x4, waiting for transfers between devices, along(): return lax.ppermute(x, 'gy', pairs)  33.8 us
    ppermute x14, starting transfers between devices, local(): pieces[s].append(lax.ppermute(x, 'gx', pairs) if k else x)  22.7 us
    unnamed x42, local copies, waits for them, and re-layouts  14.1 us
    pallas_call x4, Pallas kernels, project(): call(functools.partial(project_body, jobs=listed, share=share), [VMEM] *...  12.3 us
    all_to_all x2, starting transfers between devices, local(): pieces[s].append(lax.all_to_all(laid[0], 'gx', 0, 0, tiled=True))  11.8 us
    pallas_call x4, Pallas kernels, finish(): call(body, [SMEM, SMEM, VMEM, VMEM] + [VMEM] * len(codes), [VMEM] * len(s...  7.42 us
    ppermute x4, starting transfers between devices, along(): return lax.ppermute(x, 'gy', pairs)  6.48 us
    pallas_call x2, Pallas kernels, place(): call(functools.partial(place_body, stages=stages, modes=modes, share=shar...  5.36 us
  transfers between devices with their start and end apart: 26, of which 9 were waited for; matrix products, arithmetic and copies ran while one was open for 0% of the time, Pallas kernels for 19%

profile of v3, /device:TPU:0, one launch (start us, length us, event | category | flops | bytes accessed | tf_op | source)
XLA Modules:
  0.0 130.1 jit_solution(8173082198068120816)
XLA Ops:
  0.7 1.4 %constant_dynamic-slice_fusion.1 = (bf16[1024,256]{1,0:T(8,128)(2,1)S(1)}, bf16[1024,256]{1,0:T(8,128)(2,1)S(1)}) fusion(bf16[1024,2048]{1,0:T(8,128)(2,1)} %w_ref.1, s32[]{:T(128)S(6)} %select_n.24, s32[]{:T(128)S(6)} %select_n.25), kind=kLoop, calls=%fused_computation.2 | loop fusion | bytes 2097160 | tf_op jit(solution)/shard_map/dynamic_slice | solution.py:307
  3.2 2.2 %copy-done.3 = bf16[1024,2048]{1,0:T(8,128)(2,1)S(1)} copy-done((bf16[1024,2048]{1,0:T(8,128)(2,1)S(1)}, bf16[1024,2048]{1,0:T(8,128)(2,1)}, u32[]{:S(2)}) %copy-start.3) | copy-done | bytes 4194328
  5.4 1.7 %shard_map.68 = (bf16[16,32,1024]{2,1,0:T(8,128)(2,1)S(1)}, bf16[16,32,1024]{2,1,0:T(8,128)(2,1)S(1)}, bf16[16,32,1024]{2,1,0:T(8,128)(2,1)}, bf16[1024,512]{1,0...) custom-call(bf16[16,128,1024]{2,1,0:T(8,128)(2,1)S(1)} %bitcast.2, ...), custom_call_target="tpu_custom_call" | custom-call | flops 1000000 | bytes 12582912 | tf_op jit(solution)/shard_map/pallas_call | solution.py:82
  8.9 1.1 collective-permute-done.3.refs_6_
  10.0 1.5 %collective-permute-done.5.refs_1_.refs_4_ = bf16[16,32,1024]{2,1,0:T(8,128)(2,1)S(1)} collective-permute-done((bf16[16,32,1024]{2,1,0:T(8,128)(2,1)S(1)}, bf16[16,32,1024]{2,1,0:T(8,128)(2,1)S(1)}, u32[]{:S(2)}, u32[]{:S(2)}) %collective-permute-start.5) | collective-permute-done | bytes 1048608 | tf_op jit(solution)/shard_map/ppermute | solution.py:295
  11.5 1.5 %collective-permute-done.6.refs_4_.refs_1_ = bf16[16,32,1024]{2,1,0:T(8,128)(2,1)S(1)} collective-permute-done((bf16[16,32,1024]{2,1,0:T(8,128)(2,1)S(1)}, bf16[16,32,1024]{2,1,0:T(8,128)(2,1)S(1)}, u32[]{:S(2)}, u32[]{:S(2)}) %collective-permute-start.6) | collective-permute-done | bytes 1048608 | tf_op jit(solution)/shard_map/ppermute | solution.py:295
  13.0 2.7 %shard_map.71 = (s16[528,512]{1,0:T(8,128)(2,1)S(1)}, f32[512,512]{1,0:T(8,128)S(1)}) custom-call(bf16[16,128,1024]{2,1,0:T(8,128)(2,1)S(1)} %bitcast.4, bf16[16,32,1024]{2,1,0:T(8,128)(2,1)S(1)} %collective-permute-done.5.refs_1_.refs_4_, bf16[1024,512]{1,0:T(8,128)(2,1)S(1)} %get-tuple-element.34.refs_2_, ...), custom_call_target="tpu_custom_call" | custom-call | flops 2147483648 | bytes 3178496 | tf_op jit(solution)/shard_map/pallas_call | solution.py:142
  15.8 2.9 %collective-permute-start.15 = (s16[528,512]{1,0:T(8,128)(2,1)S(1)}, s16[528,512]{1,0:T(8,128)(2,1)S(1)}, u32[]{:S(2)}, u32[]{:S(2)}) collective-permute-start(s16[528,512]{1,0:T(8,128)(2,1)S(1)} %get-tuple-element.51), channel_id=1, source_target_pairs={{0,2},{1,3},{2,0},{3,1},{4,6},{5,7},{6,4},{7,5},{8,10},{9,11},{10,... | collective-permute-start | bytes 1622024 | tf_op jit(solution)/shard_map/ppermute | solution.py:301
  18.7 2.7 %shard_map.74 = (s16[528,512]{1,0:T(8,128)(2,1)S(1)}, f32[512,512]{1,0:T(8,128)S(1)}) custom-call(bf16[16,128,1024]{2,1,0:T(8,128)(2,1)S(1)} %bitcast.5, bf16[16,32,1024]{2,1,0:T(8,128)(2,1)S(1)} %collective-permute-done.2.refs_4_.refs_1_, bf16[1024,512]{1,0:T(8,128)(2,1)S(1)} %get-tuple-element.34.refs_2_, ...), custom_call_target="tpu_custom_call" | custom-call | flops 2147483648 | bytes 3178496 | tf_op jit(solution)/shard_map/pallas_call | solution.py:142
  21.5 0.8 copy-done.19
  22.3 9.0 %collective-permute-done.15.rest_0_ = s16[528,512]{1,0:T(8,128)(2,1)S(1)} collective-permute-done((s16[528,512]{1,0:T(8,128)(2,1)S(1)}, s16[528,512]{1,0:T(8,128)(2,1)S(1)}, u32[]{:S(2)}, u32[]{:S(2)}) %collective-permute-start.15) | collective-permute-done | bytes 540704 | tf_op jit(solution)/shard_map/ppermute | solution.py:301
  31.3 1.8 %shard_map.75 = bf16[8,64,512]{2,1,0:T(8,128)(2,1)S(1)} custom-call(s32[8,16]{1,0:T(8,128)S(1)} %copy-done.16, s32[128]{0:T(128)S(1)} %copy-done.17, f32[1,128]{1,0:T(1,128)S(1)} %bitcast.8, f32[512,512]{1,0:T(8,128)S(1)} %get-tuple-element.50.own_ref, s16[528,512]{1,0:T(8,128)(2,1)S(1)} %collective-permute-done.15.rest_0_), custom_call_target="tpu_custom_call" | custom-call | flops 5242880 | bytes 1048576 | tf_op jit(solution)/shard_map/pallas_call | solution.py:221
  33.1 0.8 copy-done.9
  33.9 6.1 %all-to-all-start.1 = ((bf16[8,64,512]{2,1,0:T(8,128)(2,1)}), bf16[8,64,512]{2,1,0:T(8,128)(2,1)}, u32[]{:S(2)}, u32[]{:S(2)}) async-start(bf16[8,64,512]{2,1,0:T(8,128)(2,1)} %copy-done.9), calls=%async_computation.1 | async-start | bytes 1048576 | tf_op jit(solution)/shard_map/all_to_all | solution.py:339
  40.0 2.2 %copy-done.1 = bf16[2048,1024]{1,0:T(8,128)(2,1)S(1)} copy-done((bf16[2048,1024]{1,0:T(8,128)(2,1)S(1)}, bf16[2048,1024]{1,0:T(8,128)(2,1)}, u32[]{:S(2)}) %copy-start.1) | copy-done | bytes 4194328
  42.2 1.2 copy-done.5
  43.4 1.2 copy-done.7
  44.7 1.2 copy-done.11
  45.9 5.0 %shard_map.69 = (s16[528,512]{1,0:T(8,128)(2,1)S(1)}, f32[512,512]{1,0:T(8,128)S(1)}, f32[512,512]{1,0:T(8,128)S(1)}) custom-call(bf16[16,128,1024]{2,1,0:T(8,128)(2,1)S(1)} %bitcast.6, bf16[16,32,1024]{2,1,0:T(8,128)(2,1)} %collective-permute-done.refs_1_, bf16[1024,512]{1,0:T(8,128)(2,1)S(1)} %get-tuple-element.34.refs_2_, ...), custom_call_target="tpu_custom_call" | custom-call | flops 3221225472 | bytes 5275648 | tf_op jit(solution)/shard_map/pallas_call | solution.py:142
  50.9 1.0 copy-done.12
  51.9 1.5 %collective-permute-start.4 = (s16[528,512]{1,0:T(8,128)(2,1)S(1)}, s16[528,512]{1,0:T(8,128)(2,1)S(1)}, u32[]{:S(2)}, u32[]{:S(2)}) collective-permute-start(s16[528,512]{1,0:T(8,128)(2,1)S(1)} %get-tuple-element.39), channel_id=1, source_target_pairs={{0,2},{1,3},{2,0},{3,1},{4,6},{5,7},{6,4},{7,5},{8,10},{9,11},{10,... | collective-permute-start | bytes 1622024 | tf_op jit(solution)/shard_map/ppermute | solution.py:301
  53.4 11.7 %collective-permute-done.4.rest_0_ = s16[528,512]{1,0:T(8,128)(2,1)S(1)} collective-permute-done((s16[528,512]{1,0:T(8,128)(2,1)S(1)}, s16[528,512]{1,0:T(8,128)(2,1)S(1)}, u32[]{:S(2)}, u32[]{:S(2)}) %collective-permute-start.4) | collective-permute-done | bytes 540704 | tf_op jit(solution)/shard_map/ppermute | solution.py:301
  65.1 1.8 %shard_map.70 = bf16[8,64,512]{2,1,0:T(8,128)(2,1)S(1)} custom-call(s32[8,16]{1,0:T(8,128)S(1)} %copy-done.16, s32[128]{0:T(128)S(1)} %copy-done.17, f32[1,128]{1,0:T(1,128)S(1)} %bitcast.9, f32[512,512]{1,0:T(8,128)S(1)} %get-tuple-element.38.own_ref, s16[528,512]{1,0:T(8,128)(2,1)S(1)} %collective-permute-done.4.rest_0_), custom_call_target="tpu_custom_call" | custom-call | flops 5242880 | bytes 1048576 | tf_op jit(solution)/shard_map/pallas_call | solution.py:221
  66.9 0.8 copy-done.8
  67.7 5.7 %all-to-all-start = ((bf16[8,64,512]{2,1,0:T(8,128)(2,1)}), bf16[8,64,512]{2,1,0:T(8,128)(2,1)}, u32[]{:S(2)}, u32[]{:S(2)}) async-start(bf16[8,64,512]{2,1,0:T(8,128)(2,1)} %copy-done.8), calls=%async_computation | async-start | bytes 1048576 | tf_op jit(solution)/shard_map/all_to_all | solution.py:339
  73.4 2.2 %copy-done.2 = bf16[2048,1024]{1,0:T(8,128)(2,1)S(1)} copy-done((bf16[2048,1024]{1,0:T(8,128)(2,1)S(1)}, bf16[2048,1024]{1,0:T(8,128)(2,1)}, u32[]{:S(2)}) %copy-start.2) | copy-done | bytes 4194328
  75.6 1.8 %shard_map.72 = s16[528,512]{1,0:T(8,128)(2,1)S(1)} custom-call(bf16[16,128,1024]{2,1,0:T(8,128)(2,1)S(1)} %bitcast.7, bf16[16,32,1024]{2,1,0:T(8,128)(2,1)S(1)} %collective-permute-done.6.refs_4_.refs_1_, bf16[1024,512]{1,0:T(8,128)(2,1)S(1)} %get-tuple-element.34.refs_2_, bf16[1024,512]{1,0:T(8,128)(2,1)S(1)} %collective-permute-done.1.refs_3_), custom_call_target="tpu_custom_call" | custom-call | flops 1073741824 | bytes 1081344 | tf_op jit(solution)/shard_map/pallas_call | solution.py:142
  77.4 1.5 %collective-permute-start.7 = (s16[528,512]{1,0:T(8,128)(2,1)S(1)}, s16[528,512]{1,0:T(8,128)(2,1)S(1)}, u32[]{:S(2)}, u32[]{:S(2)}) collective-permute-start(s16[528,512]{1,0:T(8,128)(2,1)S(1)} %shard_map.72), channel_id=1, source_target_pairs={{0,2},{1,3},{2,0},{3,1},{4,6},{5,7},{6,4},{7,5},{8,10},{9,11},{10,... | collective-permute-start | bytes 1622024 | tf_op jit(solution)/shard_map/ppermute | solution.py:301
  79.5 13.1 %collective-permute-done.7.rest_0_ = s16[528,512]{1,0:T(8,128)(2,1)S(1)} collective-permute-done((s16[528,512]{1,0:T(8,128)(2,1)S(1)}, s16[528,512]{1,0:T(8,128)(2,1)S(1)}, u32[]{:S(2)}, u32[]{:S(2)}) %collective-permute-start.7) | collective-permute-done | bytes 540704 | tf_op jit(solution)/shard_map/ppermute | solution.py:301
  92.6 1.9 %shard_map.73 = (bf16[64,512]{1,0:T(8,128)(2,1)S(1)}, bf16[64,512]{1,0:T(8,128)(2,1)S(1)}, bf16[64,512]{1,0:T(8,128)(2,1)S(1)}, bf16[64,512]{1,0:T(8,128)(2,1)S(...) custom-call(s32[8,16]{1,0:T(8,128)S(1)} %copy-done.16, ...), custom_call_target="tpu_custom_call" | custom-call | flops 5242880 | bytes 1048576 | tf_op jit(solution)/shard_map/pallas_call | solution.py:221
  94.5 2.1 %collective-permute-start.8 = (bf16[64,512]{1,0:T(8,128)(2,1)S(1)}, bf16[64,512]{1,0:T(8,128)(2,1)S(1)}, u32[]{:S(2)}, u32[]{:S(2)}) collective-permute-start(bf16[64,512]{1,0:T(8,128)(2,1)S(1)} %get-tuple-element.43), channel_id=1, source_target_pairs={{0,4},{4,8},{8,12},{12,16},{16,20},{20,24},{24,28},{28,0},{1,5},{5... | collective-permute-start | bytes 196616 | tf_op jit(solution)/shard_map/ppermute | solution.py:343
  96.6 1.5 %collective-permute-start.9 = (bf16[64,512]{1,0:T(8,128)(2,1)S(1)}, bf16[64,512]{1,0:T(8,128)(2,1)S(1)}, u32[]{:S(2)}, u32[]{:S(2)}) collective-permute-start(bf16[64,512]{1,0:T(8,128)(2,1)S(1)} %get-tuple-element.44), channel_id=1, source_target_pairs={{0,8},{4,12},{8,16},{12,20},{16,24},{20,28},{24,0},{28,4},{1,9},{5... | collective-permute-start | bytes 196616 | tf_op jit(solution)/shard_map/ppermute | solution.py:343
  98.1 2.4 %collective-permute-start.10 = (bf16[64,512]{1,0:T(8,128)(2,1)S(1)}, bf16[64,512]{1,0:T(8,128)(2,1)S(1)}, u32[]{:S(2)}, u32[]{:S(2)}) collective-permute-start(bf16[64,512]{1,0:T(8,128)(2,1)S(1)} %get-tuple-element.45), channel_id=1, source_target_pairs={{0,12},{4,16},{8,20},{12,24},{16,28},{20,0},{24,4},{28,8},{1,13},{... | collective-permute-start | bytes 196616 | tf_op jit(solution)/shard_map/ppermute | solution.py:343
  100.4 1.5 %collective-permute-start.11 = (bf16[64,512]{1,0:T(8,128)(2,1)S(1)}, bf16[64,512]{1,0:T(8,128)(2,1)S(1)}, u32[]{:S(2)}, u32[]{:S(2)}) collective-permute-start(bf16[64,512]{1,0:T(8,128)(2,1)S(1)} %get-tuple-element.46), channel_id=1, source_target_pairs={{0,16},{4,20},{8,24},{12,28},{16,0},{20,4},{24,8},{28,12},{1,17},{... | collective-permute-start | bytes 196616 | tf_op jit(solution)/shard_map/ppermute | solution.py:343
  101.9 2.5 %collective-permute-start.12 = (bf16[64,512]{1,0:T(8,128)(2,1)S(1)}, bf16[64,512]{1,0:T(8,128)(2,1)S(1)}, u32[]{:S(2)}, u32[]{:S(2)}) collective-permute-start(bf16[64,512]{1,0:T(8,128)(2,1)S(1)} %get-tuple-element.47), channel_id=1, source_target_pairs={{0,20},{4,24},{8,28},{12,0},{16,4},{20,8},{24,12},{28,16},{1,21},{... | collective-permute-start | bytes 196616 | tf_op jit(solution)/shard_map/ppermute | solution.py:343
  104.4 1.9 %shard_map.76 = (bf16[64,512]{1,0:T(8,128)(2,1)S(1)}, bf16[64,512]{1,0:T(8,128)(2,1)S(1)}, bf16[64,512]{1,0:T(8,128)(2,1)S(1)}, bf16[64,512]{1,0:T(8,128)(2,1)S(...) custom-call(s32[8,16]{1,0:T(8,128)S(1)} %copy-done.16, ...), custom_call_target="tpu_custom_call" | custom-call | flops 5242880 | bytes 1048576 | tf_op jit(solution)/shard_map/pallas_call | solution.py:221
  106.3 1.5 %collective-permute-start.13 = (bf16[64,512]{1,0:T(8,128)(2,1)S(1)}, bf16[64,512]{1,0:T(8,128)(2,1)S(1)}, u32[]{:S(2)}, u32[]{:S(2)}) collective-permute-start(bf16[64,512]{1,0:T(8,128)(2,1)S(1)} %get-tuple-element.48), channel_id=1, source_target_pairs={{0,24},{4,28},{8,0},{12,4},{16,8},{20,12},{24,16},{28,20},{1,25},{... | collective-permute-start | bytes 196616 | tf_op jit(solution)/shard_map/ppermute | solution.py:343
  107.8 1.3 %collective-permute-start.14 = (bf16[64,512]{1,0:T(8,128)(2,1)S(1)}, bf16[64,512]{1,0:T(8,128)(2,1)S(1)}, u32[]{:S(2)}, u32[]{:S(2)}) collective-permute-start(bf16[64,512]{1,0:T(8,128)(2,1)S(1)} %get-tuple-element.49), channel_id=1, source_target_pairs={{0,28},{4,0},{8,4},{12,8},{16,12},{20,16},{24,20},{28,24},{1,29},{... | collective-permute-start | bytes 196616 | tf_op jit(solution)/shard_map/ppermute | solution.py:343
  109.1 0.7 collective-permute-start.17
  109.8 0.6 collective-permute-start.18
  110.4 1.9 %collective-permute-start.19 = (bf16[64,512]{1,0:T(8,128)(2,1)S(1)}, bf16[64,512]{1,0:T(8,128)(2,1)S(1)}, u32[]{:S(2)}, u32[]{:S(2)}) collective-permute-start(bf16[64,512]{1,0:T(8,128)(2,1)S(1)} %get-tuple-element.57), channel_id=1, source_target_pairs={{0,12},{4,16},{8,20},{12,24},{16,28},{20,0},{24,4},{28,8},{1,13},{... | collective-permute-start | bytes 196616 | tf_op jit(solution)/shard_map/ppermute | solution.py:343
  112.3 2.9 %collective-permute-start.20 = (bf16[64,512]{1,0:T(8,128)(2,1)S(1)}, bf16[64,512]{1,0:T(8,128)(2,1)S(1)}, u32[]{:S(2)}, u32[]{:S(2)}) collective-permute-start(bf16[64,512]{1,0:T(8,128)(2,1)S(1)} %get-tuple-element.58), channel_id=1, source_target_pairs={{0,16},{4,20},{8,24},{12,28},{16,0},{20,4},{24,8},{28,12},{1,17},{... | collective-permute-start | bytes 196616 | tf_op jit(solution)/shard_map/ppermute | solution.py:343
  115.5 1.2 collective-permute-done.17.refs_10_
  116.7 3.5 %collective-permute-start.22 = (bf16[64,512]{1,0:T(8,128)(2,1)S(1)}, bf16[64,512]{1,0:T(8,128)(2,1)S(1)}, u32[]{:S(2)}, u32[]{:S(2)}) collective-permute-start(bf16[64,512]{1,0:T(8,128)(2,1)S(1)} %get-tuple-element.60), channel_id=1, source_target_pairs={{0,24},{4,28},{8,0},{12,4},{16,8},{20,12},{24,16},{28,20},{1,25},{... | collective-permute-start | bytes 196616 | tf_op jit(solution)/shard_map/ppermute | solution.py:343
  120.4 1.7 %collective-permute-done.22.refs_15_ = bf16[64,512]{1,0:T(8,128)(2,1)S(1)} collective-permute-done((bf16[64,512]{1,0:T(8,128)(2,1)S(1)}, bf16[64,512]{1,0:T(8,128)(2,1)S(1)}, u32[]{:S(2)}, u32[]{:S(2)}) %collective-permute-start.22) | collective-permute-done | bytes 65568 | tf_op jit(solution)/shard_map/ppermute | solution.py:343
  122.1 2.4 %collective-permute-done.23.refs_16_ = bf16[64,512]{1,0:T(8,128)(2,1)S(1)} collective-permute-done((bf16[64,512]{1,0:T(8,128)(2,1)S(1)}, bf16[64,512]{1,0:T(8,128)(2,1)S(1)}, u32[]{:S(2)}, u32[]{:S(2)}) %collective-permute-start.23) | collective-permute-done | bytes 65568 | tf_op jit(solution)/shard_map/ppermute | solution.py:343
  124.5 3.2 %shard_map.77 = (bf16[2048,256]{1,0:T(8,128)(2,1)}, bf16[2048,256]{1,0:T(8,128)(2,1)}) custom-call(s32[8,16]{1,0:T(8,128)S(1)} %copy-done.16, bf16[64,512]{1,0:T(8,128)(2,1)S(1)} %get-tuple-element.42.refs_0_, bf16[64,512]{1,0:T(8,128)(2,1)S(1)} %collective-permute-done.8.refs_1_, bf16[64,512]{1,0:T(8,128)(2,1)S(1)} %collective-permute-done.9.refs_2_, ...), custom_call_target="tpu_custom_call" | custom-call | flops 1000000 | bytes 4194304 | tf_op jit(solution)/shard_map/pallas_call | solution.py:267
  127.7 2.2 %shard_map.78 = (bf16[2048,256]{1,0:T(8,128)(2,1)}, bf16[2048,256]{1,0:T(8,128)(2,1)}) custom-call(s32[8,16]{1,0:T(8,128)S(1)} %copy-done.16, bf16[8,64,512]{2,1,0:T(8,128)(2,1)} %all-to-all-done.refs_0_, bf16[2048,256]{1,0:T(8,128)(2,1)} %get-tuple-element.62.refs_1_, ...), custom_call_target="tpu_custom_call", output_to_operand_aliasing={{0}: (2, {}), {1}: (3, {})} | custom-call | flops 1000000 | bytes 4194304 | tf_op jit(solution)/shard_map/pallas_call | solution.py:267
  (60 shorter events, 4.0 us)
Async XLA Ops:
  0.7 2.5 %copy-start = (bf16[2048,1024]{1,0:T(8,128)(2,1)S(1)}, bf16[2048,1024]{1,0:T(8,128)(2,1)}, u32[]{:S(2)}) copy-start(bf16[2048,1024]{1,0:T(8,128)(2,1)} %param.5) | copy-start | bytes 12582916
  2.2 6.3 %collective-permute-start.1 = (bf16[1024,512]{1,0:T(8,128)(2,1)S(1)}, bf16[1024,512]{1,0:T(8,128)(2,1)S(1)}, u32[]{:S(2)}, u32[]{:S(2)}) collective-permute-start(bf16[1024,512]{1,0:T(8,128)(2,1)S(1)} %pad_maximum_fusion), channel_id=1, source_target_pairs={{0,1},{1,0},{2,3},{3,2},{4,5},{5,4},{6,7},{7,6},{8,9},{9,8},{10,11... | collective-permute-start | bytes 3145736 | tf_op jit(solution)/shard_map/ppermute | solution.py:295
  3.2 2.2 %copy-start.3 = (bf16[1024,2048]{1,0:T(8,128)(2,1)S(1)}, bf16[1024,2048]{1,0:T(8,128)(2,1)}, u32[]{:S(2)}) copy-start(bf16[1024,2048]{1,0:T(8,128)(2,1)} %w_ref.1) | copy-start | bytes 12582916
  7.1 11.6 %copy-start.4 = (bf16[1024,512]{1,0:T(8,128)(2,1)}, bf16[1024,512]{1,0:T(8,128)(2,1)S(1)}, u32[]{:S(2)}) copy-start(bf16[1024,512]{1,0:T(8,128)(2,1)S(1)} %get-tuple-element.36.refs_5_) | copy-start | bytes 3145732
  7.2 2.8 %collective-permute-start.3 = (bf16[1024,512]{1,0:T(8,128)(2,1)S(1)}, bf16[1024,512]{1,0:T(8,128)(2,1)S(1)}, u32[]{:S(2)}, u32[]{:S(2)}) collective-permute-start(bf16[1024,512]{1,0:T(8,128)(2,1)S(1)} %get-tuple-element.37), channel_id=1, source_target_pairs={{0,1},{1,0},{2,3},{3,2},{4,5},{5,4},{6,7},{7,6},{8,9},{9,8},{10,11... | collective-permute-start | bytes 3145736 | tf_op jit(solution)/shard_map/ppermute | solution.py:295
  7.7 3.8 %collective-permute-start.5 = (bf16[16,32,1024]{2,1,0:T(8,128)(2,1)S(1)}, bf16[16,32,1024]{2,1,0:T(8,128)(2,1)S(1)}, u32[]{:S(2)}, u32[]{:S(2)}) collective-permute-start(bf16[16,32,1024]{2,1,0:T(8,128)(2,1)S(1)} %get-tuple-element.40), channel_id=1, source_target_pairs={{0,1},{1,0},{2,3},{3,2},{4,5},{5,4},{6,7},{7,6},{8,9},{9,8},{10,11... | collective-permute-start | bytes 3145736 | tf_op jit(solution)/shard_map/ppermute | solution.py:295
  7.9 5.1 %collective-permute-start.6 = (bf16[16,32,1024]{2,1,0:T(8,128)(2,1)S(1)}, bf16[16,32,1024]{2,1,0:T(8,128)(2,1)S(1)}, u32[]{:S(2)}, u32[]{:S(2)}) collective-permute-start(bf16[16,32,1024]{2,1,0:T(8,128)(2,1)S(1)} %slice.4), channel_id=1, source_target_pairs={{0,1},{1,0},{2,3},{3,2},{4,5},{5,4},{6,7},{7,6},{8,9},{9,8},{10,11... | collective-permute-start | bytes 3145736 | tf_op jit(solution)/shard_map/ppermute | solution.py:295
  8.4 10.3 %collective-permute-start.2 = (bf16[16,32,1024]{2,1,0:T(8,128)(2,1)S(1)}, bf16[16,32,1024]{2,1,0:T(8,128)(2,1)S(1)}, u32[]{:S(2)}, u32[]{:S(2)}) collective-permute-start(bf16[16,32,1024]{2,1,0:T(8,128)(2,1)S(1)} %get-tuple-element.35), channel_id=1, source_target_pairs={{0,1},{1,0},{2,3},{3,2},{4,5},{5,4},{6,7},{7,6},{8,9},{9,8},{10,11... | collective-permute-start | bytes 3145736 | tf_op jit(solution)/shard_map/ppermute | solution.py:295
  8.5 31.6 %collective-permute-start = (bf16[16,32,1024]{2,1,0:T(8,128)(2,1)}, bf16[16,32,1024]{2,1,0:T(8,128)(2,1)}, u32[]{:S(2)}, u32[]{:S(2)}) collective-permute-start(bf16[16,32,1024]{2,1,0:T(8,128)(2,1)} %get-tuple-element.33), channel_id=1, source_target_pairs={{0,1},{1,0},{2,3},{3,2},{4,5},{5,4},{6,7},{7,6},{8,9},{9,8},{10,11... | collective-permute-start | bytes 3145736 | tf_op jit(solution)/shard_map/ppermute | solution.py:295
  10.0 8.7 %copy-start.6 = (bf16[1024,512]{1,0:T(8,128)(2,1)}, bf16[1024,512]{1,0:T(8,128)(2,1)S(1)}, u32[]{:S(2)}) copy-start(bf16[1024,512]{1,0:T(8,128)(2,1)S(1)} %collective-permute-done.3.refs_6_) | copy-start | bytes 3145732
  15.7 5.7 %copy-start.14 = (f32[512,512]{1,0:T(8,128)}, f32[512,512]{1,0:T(8,128)S(1)}, u32[]{:S(2)}) copy-start(f32[512,512]{1,0:T(8,128)S(1)} %get-tuple-element.41.own_ref) | copy-start | bytes 3145732
  15.7 15.5 %copy-start.16 = (s32[8,16]{1,0:T(8,128)S(1)}, s32[8,16]{1,0:T(8,128)}, u32[]{:S(2)}) copy-start(s32[8,16]{1,0:T(8,128)} %deal_ref.11) | copy-start | bytes 1540
  15.8 15.5 %copy-start.17 = (s32[128]{0:T(128)S(1)}, s32[128]{0:T(128)}, u32[]{:S(2)}) copy-start(s32[128]{0:T(128)} %limit_ref.7) | copy-start | bytes 1540
  15.8 15.5 %copy-start.18 = (f32[128]{0:T(128)S(1)}, f32[128]{0:T(128)}, u32[]{:S(2)}) copy-start(f32[128]{0:T(128)} %param.7) | copy-start | bytes 1540
  15.8 15.5 %collective-permute-start.15 = (s16[528,512]{1,0:T(8,128)(2,1)S(1)}, s16[528,512]{1,0:T(8,128)(2,1)S(1)}, u32[]{:S(2)}, u32[]{:S(2)}) collective-permute-start(s16[528,512]{1,0:T(8,128)(2,1)S(1)} %get-tuple-element.51), channel_id=1, source_target_pairs={{0,2},{1,3},{2,0},{3,1},{4,6},{5,7},{6,4},{7,5},{8,10},{9,11},{10,... | collective-permute-start | bytes 1622024 | tf_op jit(solution)/shard_map/ppermute | solution.py:301
  18.7 2.8 %copy-start.10 = (bf16[16,32,1024]{2,1,0:T(8,128)(2,1)}, bf16[16,32,1024]{2,1,0:T(8,128)(2,1)S(1)}, u32[]{:S(2)}) copy-start(bf16[16,32,1024]{2,1,0:T(8,128)(2,1)S(1)} %collective-permute-done.2.refs_4_.refs_1_) | copy-start | bytes 3145732
  21.5 0.8 copy-start.19
  33.1 0.8 copy-start.9
  33.9 33.8 %all-to-all-start.1 = ((bf16[8,64,512]{2,1,0:T(8,128)(2,1)}), bf16[8,64,512]{2,1,0:T(8,128)(2,1)}, u32[]{:S(2)}, u32[]{:S(2)}) async-start(bf16[8,64,512]{2,1,0:T(8,128)(2,1)} %copy-done.9), calls=%async_computation.1 | async-start | bytes 1048576 | tf_op jit(solution)/shard_map/all_to_all | solution.py:339
  40.0 2.2 %copy-start.1 = (bf16[2048,1024]{1,0:T(8,128)(2,1)S(1)}, bf16[2048,1024]{1,0:T(8,128)(2,1)}, u32[]{:S(2)}) copy-start(bf16[2048,1024]{1,0:T(8,128)(2,1)} %param.5) | copy-start | bytes 12582916
  42.2 1.2 copy-start.5
  43.4 1.2 copy-start.7
  44.7 1.2 copy-start.11
  50.9 1.0 copy-start.12
  51.9 13.2 %collective-permute-start.4 = (s16[528,512]{1,0:T(8,128)(2,1)S(1)}, s16[528,512]{1,0:T(8,128)(2,1)S(1)}, u32[]{:S(2)}, u32[]{:S(2)}) collective-permute-start(s16[528,512]{1,0:T(8,128)(2,1)S(1)} %get-tuple-element.39), channel_id=1, source_target_pairs={{0,2},{1,3},{2,0},{3,1},{4,6},{5,7},{6,4},{7,5},{8,10},{9,11},{10,... | collective-permute-start | bytes 1622024 | tf_op jit(solution)/shard_map/ppermute | solution.py:301
  66.9 0.8 copy-start.8
  67.7 59.9 %all-to-all-start = ((bf16[8,64,512]{2,1,0:T(8,128)(2,1)}), bf16[8,64,512]{2,1,0:T(8,128)(2,1)}, u32[]{:S(2)}, u32[]{:S(2)}) async-start(bf16[8,64,512]{2,1,0:T(8,128)(2,1)} %copy-done.8), calls=%async_computation | async-start | bytes 1048576 | tf_op jit(solution)/shard_map/all_to_all | solution.py:339
  73.4 2.2 %copy-start.2 = (bf16[2048,1024]{1,0:T(8,128)(2,1)S(1)}, bf16[2048,1024]{1,0:T(8,128)(2,1)}, u32[]{:S(2)}) copy-start(bf16[2048,1024]{1,0:T(8,128)(2,1)} %param.5) | copy-start | bytes 12582916
  75.6 3.3 %copy-start.20 = (s16[528,512]{1,0:T(8,128)(2,1)S(1)}, s16[528,512]{1,0:T(8,128)(2,1)}, u32[]{:S(2)}) copy-start(s16[528,512]{1,0:T(8,128)(2,1)} %copy-done.19) | copy-start | bytes 1622020
  75.6 17.0 %copy-start.15 = (f32[512,512]{1,0:T(8,128)S(1)}, f32[512,512]{1,0:T(8,128)}, u32[]{:S(2)}) copy-start(f32[512,512]{1,0:T(8,128)} %copy-done.14) | copy-start | bytes 3145732
  75.6 28.7 %copy-start.13 = (f32[512,512]{1,0:T(8,128)S(1)}, f32[512,512]{1,0:T(8,128)}, u32[]{:S(2)}) copy-start(f32[512,512]{1,0:T(8,128)} %copy-done.12) | copy-start | bytes 3145732
  77.4 15.2 %collective-permute-start.7 = (s16[528,512]{1,0:T(8,128)(2,1)S(1)}, s16[528,512]{1,0:T(8,128)(2,1)S(1)}, u32[]{:S(2)}, u32[]{:S(2)}) collective-permute-start(s16[528,512]{1,0:T(8,128)(2,1)S(1)} %shard_map.72), channel_id=1, source_target_pairs={{0,2},{1,3},{2,0},{3,1},{4,6},{5,7},{6,4},{7,5},{8,10},{9,11},{10,... | collective-permute-start | bytes 1622024 | tf_op jit(solution)/shard_map/ppermute | solution.py:301
  79.0 22.9 %collective-permute-start.16 = (s16[528,512]{1,0:T(8,128)(2,1)S(1)}, s16[528,512]{1,0:T(8,128)(2,1)S(1)}, u32[]{:S(2)}, u32[]{:S(2)}) collective-permute-start(s16[528,512]{1,0:T(8,128)(2,1)S(1)} %copy-done.20), channel_id=1, source_target_pairs={{0,2},{1,3},{2,0},{3,1},{4,6},{5,7},{6,4},{7,5},{8,10},{9,11},{10,... | collective-permute-start | bytes 1622024 | tf_op jit(solution)/shard_map/ppermute | solution.py:301
  94.5 11.7 %collective-permute-start.8 = (bf16[64,512]{1,0:T(8,128)(2,1)S(1)}, bf16[64,512]{1,0:T(8,128)(2,1)S(1)}, u32[]{:S(2)}, u32[]{:S(2)}) collective-permute-start(bf16[64,512]{1,0:T(8,128)(2,1)S(1)} %get-tuple-element.43), channel_id=1, source_target_pairs={{0,4},{4,8},{8,12},{12,16},{16,20},{20,24},{24,28},{28,0},{1,5},{5... | collective-permute-start | bytes 196616 | tf_op jit(solution)/shard_map/ppermute | solution.py:343
  96.6 11.2 %collective-permute-start.9 = (bf16[64,512]{1,0:T(8,128)(2,1)S(1)}, bf16[64,512]{1,0:T(8,128)(2,1)S(1)}, u32[]{:S(2)}, u32[]{:S(2)}) collective-permute-start(bf16[64,512]{1,0:T(8,128)(2,1)S(1)} %get-tuple-element.44), channel_id=1, source_target_pairs={{0,8},{4,12},{8,16},{12,20},{16,24},{20,28},{24,0},{28,4},{1,9},{5... | collective-permute-start | bytes 196616 | tf_op jit(solution)/shard_map/ppermute | solution.py:343
  98.1 11.1 %collective-permute-start.10 = (bf16[64,512]{1,0:T(8,128)(2,1)S(1)}, bf16[64,512]{1,0:T(8,128)(2,1)S(1)}, u32[]{:S(2)}, u32[]{:S(2)}) collective-permute-start(bf16[64,512]{1,0:T(8,128)(2,1)S(1)} %get-tuple-element.45), channel_id=1, source_target_pairs={{0,12},{4,16},{8,20},{12,24},{16,28},{20,0},{24,4},{28,8},{1,13},{... | collective-permute-start | bytes 196616 | tf_op jit(solution)/shard_map/ppermute | solution.py:343
  100.4 9.4 %collective-permute-start.11 = (bf16[64,512]{1,0:T(8,128)(2,1)S(1)}, bf16[64,512]{1,0:T(8,128)(2,1)S(1)}, u32[]{:S(2)}, u32[]{:S(2)}) collective-permute-start(bf16[64,512]{1,0:T(8,128)(2,1)S(1)} %get-tuple-element.46), channel_id=1, source_target_pairs={{0,16},{4,20},{8,24},{12,28},{16,0},{20,4},{24,8},{28,12},{1,17},{... | collective-permute-start | bytes 196616 | tf_op jit(solution)/shard_map/ppermute | solution.py:343
  101.9 8.5 %collective-permute-start.12 = (bf16[64,512]{1,0:T(8,128)(2,1)S(1)}, bf16[64,512]{1,0:T(8,128)(2,1)S(1)}, u32[]{:S(2)}, u32[]{:S(2)}) collective-permute-start(bf16[64,512]{1,0:T(8,128)(2,1)S(1)} %get-tuple-element.47), channel_id=1, source_target_pairs={{0,20},{4,24},{8,28},{12,0},{16,4},{20,8},{24,12},{28,16},{1,21},{... | collective-permute-start | bytes 196616 | tf_op jit(solution)/shard_map/ppermute | solution.py:343
  106.3 6.0 %collective-permute-start.13 = (bf16[64,512]{1,0:T(8,128)(2,1)S(1)}, bf16[64,512]{1,0:T(8,128)(2,1)S(1)}, u32[]{:S(2)}, u32[]{:S(2)}) collective-permute-start(bf16[64,512]{1,0:T(8,128)(2,1)S(1)} %get-tuple-element.48), channel_id=1, source_target_pairs={{0,24},{4,28},{8,0},{12,4},{16,8},{20,12},{24,16},{28,20},{1,25},{... | collective-permute-start | bytes 196616 | tf_op jit(solution)/shard_map/ppermute | solution.py:343
  107.8 7.3 %collective-permute-start.14 = (bf16[64,512]{1,0:T(8,128)(2,1)S(1)}, bf16[64,512]{1,0:T(8,128)(2,1)S(1)}, u32[]{:S(2)}, u32[]{:S(2)}) collective-permute-start(bf16[64,512]{1,0:T(8,128)(2,1)S(1)} %get-tuple-element.49), channel_id=1, source_target_pairs={{0,28},{4,0},{8,4},{12,8},{16,12},{20,16},{24,20},{28,24},{1,29},{... | collective-permute-start | bytes 196616 | tf_op jit(solution)/shard_map/ppermute | solution.py:343
  109.1 7.5 %collective-permute-start.17 = (bf16[64,512]{1,0:T(8,128)(2,1)S(1)}, bf16[64,512]{1,0:T(8,128)(2,1)S(1)}, u32[]{:S(2)}, u32[]{:S(2)}) collective-permute-start(bf16[64,512]{1,0:T(8,128)(2,1)S(1)} %get-tuple-element.55), channel_id=1, source_target_pairs={{0,4},{4,8},{8,12},{12,16},{16,20},{20,24},{24,28},{28,0},{1,5},{5... | collective-permute-start | bytes 196616 | tf_op jit(solution)/shard_map/ppermute | solution.py:343
  109.8 10.4 %collective-permute-start.18 = (bf16[64,512]{1,0:T(8,128)(2,1)S(1)}, bf16[64,512]{1,0:T(8,128)(2,1)S(1)}, u32[]{:S(2)}, u32[]{:S(2)}) collective-permute-start(bf16[64,512]{1,0:T(8,128)(2,1)S(1)} %get-tuple-element.56), channel_id=1, source_target_pairs={{0,8},{4,12},{8,16},{12,20},{16,24},{20,28},{24,0},{28,4},{1,9},{5... | collective-permute-start | bytes 196616 | tf_op jit(solution)/shard_map/ppermute | solution.py:343
  110.4 10.0 %collective-permute-start.19 = (bf16[64,512]{1,0:T(8,128)(2,1)S(1)}, bf16[64,512]{1,0:T(8,128)(2,1)S(1)}, u32[]{:S(2)}, u32[]{:S(2)}) collective-permute-start(bf16[64,512]{1,0:T(8,128)(2,1)S(1)} %get-tuple-element.57), channel_id=1, source_target_pairs={{0,12},{4,16},{8,20},{12,24},{16,28},{20,0},{24,4},{28,8},{1,13},{... | collective-permute-start | bytes 196616 | tf_op jit(solution)/shard_map/ppermute | solution.py:343
  112.3 8.2 %collective-permute-start.20 = (bf16[64,512]{1,0:T(8,128)(2,1)S(1)}, bf16[64,512]{1,0:T(8,128)(2,1)S(1)}, u32[]{:S(2)}, u32[]{:S(2)}) collective-permute-start(bf16[64,512]{1,0:T(8,128)(2,1)S(1)} %get-tuple-element.58), channel_id=1, source_target_pairs={{0,16},{4,20},{8,24},{12,28},{16,0},{20,4},{24,8},{28,12},{1,17},{... | collective-permute-start | bytes 196616 | tf_op jit(solution)/shard_map/ppermute | solution.py:343
  115.1 5.3 %collective-permute-start.21 = (bf16[64,512]{1,0:T(8,128)(2,1)S(1)}, bf16[64,512]{1,0:T(8,128)(2,1)S(1)}, u32[]{:S(2)}, u32[]{:S(2)}) collective-permute-start(bf16[64,512]{1,0:T(8,128)(2,1)S(1)} %get-tuple-element.59), channel_id=1, source_target_pairs={{0,20},{4,24},{8,28},{12,0},{16,4},{20,8},{24,12},{28,16},{1,21},{... | collective-permute-start | bytes 196616 | tf_op jit(solution)/shard_map/ppermute | solution.py:343
  116.7 5.5 %collective-permute-start.22 = (bf16[64,512]{1,0:T(8,128)(2,1)S(1)}, bf16[64,512]{1,0:T(8,128)(2,1)S(1)}, u32[]{:S(2)}, u32[]{:S(2)}) collective-permute-start(bf16[64,512]{1,0:T(8,128)(2,1)S(1)} %get-tuple-element.60), channel_id=1, source_target_pairs={{0,24},{4,28},{8,0},{12,4},{16,8},{20,12},{24,16},{28,20},{1,25},{... | collective-permute-start | bytes 196616 | tf_op jit(solution)/shard_map/ppermute | solution.py:343
  120.2 4.3 %collective-permute-start.23 = (bf16[64,512]{1,0:T(8,128)(2,1)S(1)}, bf16[64,512]{1,0:T(8,128)(2,1)S(1)}, u32[]{:S(2)}, u32[]{:S(2)}) collective-permute-start(bf16[64,512]{1,0:T(8,128)(2,1)S(1)} %get-tuple-element.61), channel_id=1, source_target_pairs={{0,28},{4,0},{8,4},{12,8},{16,12},{20,16},{24,20},{28,24},{1,29},{... | collective-permute-start | bytes 196616 | tf_op jit(solution)/shard_map/ppermute | solution.py:343
